TPU v7x, 256 devices: a whole 4x4x8 slice. The times are simulated.
256 devices in a mesh: dp: 8 (over z), expert: 32 (over y, x, core).
Axes of the slice: x: 4, y: 4, z: 8, core: 2. Of those that a mesh axis runs over, the one named last changes fastest.
Arguments:
- tokens: bfloat16 [1024, 7168], P(('dp', 'expert')), may hold values from -6 to 6
- routes: int32 [1024, 8], P(('dp', 'expert')), may hold values from 0 to 31, all different within a row; in each aligned block of 4 rows (0 to 3, 4 to 7, ...) at most 2 rows name the same one
- gate_scores: float32 [1024, 8], P(('dp', 'expert')), may hold values from 0.1 to 1
- w_gate: bfloat16 [32, 7168, 2048], P('expert', None, 'dp'), may hold values from -0.0625 to 0.0625
- w_up: bfloat16 [32, 7168, 2048], P('expert', None, 'dp'), may hold values from -0.0625 to 0.0625
- w_down: bfloat16 [32, 2048, 7168], P('expert', 'dp'), may hold values from -0.125 to 0.125
Outputs:
- mixed_out: bfloat16 [1024, 7168], P(('dp', 'expert'))
Inputs may be any that keep to these rules, and one draw needn't show every extreme that they name: `routes`: each row names 8 different experts. In the rows of one device (aligned blocks of 4 rows) no expert is named by more than 2 rows, a bound that some block reaches.
All inputs are finite; a program needn't handle non-finite values.
Results may differ from a plain program's by a relative error of at most 0.0098.
Values may be sent and summed in bfloat16 or wider, within the bound.
No kernel may reach another device: no remote copies, remote signals or barrier semaphores. Data moves between devices by JAX's collectives and lax.ppermute only.
A program may use at most 128 MiB of HBM per device.

v0:
```python
import functools

import jax
import jax.numpy as jnp
from jax import lax
from jax.experimental import pallas as pl
from jax.experimental.pallas import tpu as pltpu
from jax.sharding import Mesh, PartitionSpec as P


LANES = 128


def shift(value, axis, step):
    n = lax.axis_size(axis)
    return lax.ppermute(value, axis, [(i, (i + step) % n) for i in range(n)])


def near_gather(own, axis):
    return jnp.stack([own, shift(own, axis, -1), shift(own, axis, 2), shift(own, axis, 1)])


def near_reduce(own, succ, across, prev, axis):
    return added(own, shift(succ, axis, 1), shift(across, axis, 2), shift(prev, axis, -1))


def far_gather(own, axis):
    half = own.shape[0] // 2
    prev = shift(own, axis, 1)
    succ = shift(own, axis, -1)
    low = shift(prev[:half], axis, 1)
    high = shift(succ[half:], axis, -1)
    return own, succ, low, high, prev


def far_reduce(own, succ, low, high, prev, axis):
    half = low.shape[0]
    got_low = shift(low, axis, 1)
    got_high = shift(high, axis, -1)
    to_succ = jnp.concatenate([added(succ[:half], got_low), succ[half:]], axis=0)
    to_prev = jnp.concatenate([prev[:half], added(prev[half:], got_high)], axis=0)
    return added(own, shift(to_succ, axis, 1), shift(to_prev, axis, -1))


def added(*terms):
    total = terms[0].astype(jnp.float32)
    for term in terms[1:]:
        total = total + term.astype(jnp.float32)
    return total.astype(jnp.bfloat16)


def by_core(core, if_zero, if_one):
    return jnp.where(core == 0, if_zero, if_one)


PLACES = ((0, 0, 4), (1, 0, 4), (2, 0, 2), (2, 2, 2), (3, 0, 4))


def hidden_kernel(place_ref, *refs):
    pieces, (gate_ref, up_ref, out_ref) = refs[:20], refs[20:23]
    x_buf, w_buf, acc, named, x_sem, w_sem, named_sem = refs[23:]
    rows, width = x_buf.shape[3:]
    ff = gate_ref.shape[1]
    core, expert = place_ref[0], place_ref[1]
    for side in range(2):
        which = core if side == 0 else 1 - core
        half = pl.ds(pl.multiple_of(which * 2 * width, LANES), 2 * width)
        for k, ref in enumerate((gate_ref, up_ref)):
            pltpu.make_async_copy(
                ref.at[half, :], w_buf.at[side, :, k * ff : (k + 1) * ff], w_sem.at[side]
            ).start()
        for i in range(side * 10, side * 10 + 10):
            group = i // 5
            offset, first, count = PLACES[i % 5]
            skip = pieces[i].shape[2] - width
            pltpu.make_async_copy(
                pieces[i].at[:, :, skip : skip + width],
                x_buf.at[group, offset, first : first + count],
                x_sem.at[group, offset],
            ).start()
    for i, (offset, first, count) in enumerate(PLACES):
        pltpu.make_async_copy(
            pieces[i].at[:, :, :LANES], named.at[offset, first : first + count], named_sem
        ).start()

    def step(i, _):
        group, offset = i // 4, i % 4
        side, colour = group // 2, group % 2

        @pl.when(i % 8 == 0)
        def _():
            pltpu.make_async_copy(w_buf.at[side], w_buf.at[side], w_sem.at[side]).wait()

        there = x_buf.at[group, offset]
        pltpu.make_async_copy(there, there, x_sem.at[group, offset]).wait()
        x = x_buf[group, offset].reshape(4 * rows, width)
        w = w_buf[side, pl.ds(pl.multiple_of(colour * width, LANES), width), :]
        part = jnp.dot(x, w, preferred_element_type=jnp.float32).reshape(4, rows, 2 * ff)
        acc[colour, offset] = jnp.where(side == 0, part, part + acc[colour, offset])
        return 0

    lax.fori_loop(0, 16, step, 0)
    pltpu.make_async_copy(named, named, named_sem).wait()
    lane = lax.broadcasted_iota(jnp.int32, (LANES, ff), 0)
    chosen = ((lane == expert) | (lane == expert + LANES // 2)).astype(jnp.bfloat16)

    def finish(offset, _):
        weight = jnp.dot(
            named[offset].reshape(4 * rows, LANES), chosen, preferred_element_type=jnp.float32
        ).reshape(4, rows, ff)
        for j in range(4):
            gate = acc[0, offset, j, :, :ff] + acc[1, j, offset, :, :ff]
            up = acc[0, offset, j, :, ff:] + acc[1, j, offset, :, ff:]
            act = (gate / (1.0 + jnp.exp(-gate)) * up * weight[j]).astype(jnp.bfloat16)
            out_ref[0, offset, j] = act
            out_ref[1, j, offset] = act
        return 0

    lax.fori_loop(0, 4, finish, 0)


def hidden_call(place, own, sibling, gate_mat, up_mat):
    rows = own[0].shape[1]
    ff = gate_mat.shape[1]
    width = gate_mat.shape[0] // 4
    any_spec = pl.BlockSpec(memory_space=pl.ANY)
    return pl.pallas_call(
        hidden_kernel,
        out_shape=jax.ShapeDtypeStruct((2, 4, 4, rows, ff), jnp.bfloat16),
        in_specs=[pl.BlockSpec(memory_space=pltpu.SMEM)] + [any_spec] * 22,
        out_specs=pl.BlockSpec(memory_space=pltpu.VMEM),
        scratch_shapes=[
            pltpu.VMEM((4, 4, 4, rows, width), jnp.bfloat16),
            pltpu.VMEM((2, 2 * width, 2 * ff), jnp.bfloat16),
            pltpu.VMEM((2, 4, 4, rows, 2 * ff), jnp.float32),
            pltpu.VMEM((4, 4, rows, LANES), jnp.bfloat16),
            pltpu.SemaphoreType.DMA((4, 4)),
            pltpu.SemaphoreType.DMA((2,)),
            pltpu.SemaphoreType.DMA,
        ],
        compiler_params=pltpu.CompilerParams(vmem_limit_bytes=40 * 2**20),
        cost_estimate=pl.CostEstimate(
            flops=2 * 16 * rows * gate_mat.shape[0] * 2 * ff,
            bytes_accessed=24 * 2**20,
            transcendentals=0,
        ),
        name="hidden",
    )(place, *own, *sibling, gate_mat, up_mat)


def down_kernel(offsets, adds, place_ref, h_ref, w_ref, *refs):
    recv_ref = refs[0] if adds else None
    refs = refs[1:] if adds else refs
    count = len(offsets)
    n_out = len(refs) - 6 if adds else 1
    outs = refs[:n_out]
    w_buf, o_buf, *r_buf, w_sem, o_sem, r_sem = refs[n_out:]
    ff, width = w_buf.shape[1:]
    half = place_ref[0] if adds else 1 - place_ref[0]
    for colour in range(2):
        columns = pl.ds(pl.multiple_of((half * 2 + colour) * width, LANES), width)
        pltpu.make_async_copy(w_ref.at[:, columns], w_buf.at[colour], w_sem.at[colour]).start()
    units = [(k, colour) for k in range(count) for colour in range(2)]
    for k, colour in units if adds else ():
        pltpu.make_async_copy(recv_ref.at[k, colour], r_buf[0].at[k, colour], r_sem.at[k, colour]).start()
    steps = 2 if width % (4 * LANES) == 0 else 1
    tile = width // steps

    def copies(i):
        k, colour = units[i]
        if not adds:
            todo = [(o_buf.at[k, colour], outs[0].at[k, colour])]
        else:
            each, length = n_out // len(units), outs[0].shape[0]
            todo = [
                (o_buf.at[k, colour, length * j : length * (j + 1)], outs[i * each + j])
                for j in range(each)
            ]
        return [pltpu.make_async_copy(a, b, o_sem.at[i, j]) for j, (a, b) in enumerate(todo)]

    def unit(i, _):
        k, colour = i // 2, i % 2
        offset = k + k // 2 if count > 1 else offsets[0]

        @pl.when(k == 0)
        def _():
            pltpu.make_async_copy(w_buf.at[colour], w_buf.at[colour], w_sem.at[colour]).wait()

        if adds:
            there = r_buf[0].at[k, colour]
            pltpu.make_async_copy(there, there, r_sem.at[k, colour]).wait()
        h = h_ref[colour, offset].reshape(-1, ff)

        def column(t, _):
            at = pl.ds(pl.multiple_of(t * tile, LANES), tile)
            part = jnp.dot(h, w_buf[colour, :, at], preferred_element_type=jnp.float32)
            part = part.reshape(4, -1, tile)
            if adds:
                part = part + r_buf[0][k, colour, :, :, at].astype(jnp.float32)
            o_buf[k, colour, :, :, at] = part.astype(jnp.bfloat16)
            return 0

        lax.fori_loop(0, steps, column, 0)
        for u in range(2 * count):

            @pl.when(i == u)
            def _(u=u):
                for copy in copies(u):
                    copy.start()

        return 0

    lax.fori_loop(0, 2 * count, unit, 0)
    for u in range(2 * count):
        for copy in copies(u):
            copy.wait()


def down_call(place, hidden, down_mat, offsets, received):
    adds = received is not None
    rows, ff = hidden.shape[3:]
    width = down_mat.shape[1] // 4
    count = len(offsets)
    any_spec = pl.BlockSpec(memory_space=pl.ANY)
    whole = (count, 2, 4, rows, width)
    parts = 2 if offsets == (2,) else 1
    piece = jax.ShapeDtypeStruct((4 // parts, rows, width), jnp.bfloat16)
    moved = 2 * 2 * count * 4 * rows * width
    return pl.pallas_call(
        functools.partial(down_kernel, offsets, adds),
        out_shape=[piece] * (2 * count * parts) if adds else [jax.ShapeDtypeStruct(whole, jnp.bfloat16)],
        in_specs=[
            pl.BlockSpec(memory_space=pltpu.SMEM),
            pl.BlockSpec(memory_space=pltpu.VMEM),
            any_spec,
        ]
        + [any_spec] * adds,
        out_specs=[any_spec] * (2 * count * parts if adds else 1),
        scratch_shapes=[pltpu.VMEM((2, ff, width), jnp.bfloat16)]
        + [pltpu.VMEM(whole, jnp.bfloat16)] * (1 + adds)
        + [
            pltpu.SemaphoreType.DMA((2,)),
            pltpu.SemaphoreType.DMA((2 * count, 2)),
            pltpu.SemaphoreType.DMA((count, 2)),
        ],
        compiler_params=pltpu.CompilerParams(vmem_limit_bytes=20 * 2**20),
        cost_estimate=pl.CostEstimate(
            flops=2 * count * 8 * rows * ff * width,
            bytes_accessed=moved * (2 if adds else 1),
            transcendentals=0,
        ),
        name="down_add" if adds else "down_send",
    )(place, hidden, down_mat, *([received] if adds else []))


def step(tokens, routes, gate_scores, w_gate, w_up, w_down):
    tok_rows, model_width = tokens.shape
    half = model_width // 2
    core = lax.axis_index("c")
    expert = lax.axis_index(("y", "x", "c")).astype(jnp.int32)
    place = jnp.stack([core.astype(jnp.int32), expert])

    experts = lax.axis_size(("y", "x", "c"))
    named = routes[:, :, None] == jnp.arange(experts, dtype=jnp.int32)
    weights = jnp.sum(jnp.where(named, gate_scores[:, :, None], 0.0), axis=1)
    top = lax.reduce_precision(weights, 8, 7)
    pad = jnp.zeros((tok_rows, LANES // 2 - experts), jnp.float32)
    tile = jnp.concatenate([top, pad, weights - top, pad], axis=1).astype(jnp.bfloat16)

    first, second = tokens[:, :half], tokens[:, half:]
    mine = jnp.concatenate([tile, by_core(core, first, second)], axis=1)
    theirs = jnp.concatenate([tile, by_core(core, second, first)], axis=1)
    other = shift(theirs, "c", 1)
    block = by_core(
        core, jnp.concatenate([mine, other], axis=0), jnp.concatenate([other, mine], axis=0)
    )

    n_z = lax.axis_size("z")
    column = jnp.broadcast_to(block, (n_z, *block.shape))
    column = lax.all_to_all(column, "z", split_axis=0, concat_axis=0, tiled=True)
    column = column.reshape(-1, block.shape[1])
    cut = LANES + half // 2
    gathered = []
    for part, (near, far) in ((column[:, :cut], ("x", "y")), (column[:, cut:], ("y", "x"))):
        gathered.extend(far_gather(near_gather(part, near), far))
    swapped = [shift(piece, "c", 1) for piece in gathered]
    hidden = hidden_call(place, gathered, swapped, w_gate[0], w_up[0])

    down_mat = w_down[0]
    groups = ((2,), (0, 1, 3))
    far_sent = down_call(place, hidden, down_mat, groups[0], None)[0]
    far_got = shift(far_sent, "c", 1)
    sent = down_call(place, hidden, down_mat, groups[1], None)[0]
    across = down_call(place, hidden, down_mat, groups[0], far_got)
    got = shift(sent, "c", 1)
    others = down_call(place, hidden, down_mat, groups[1], got)
    sums = []
    for colour, (near, far) in enumerate((("x", "y"), ("y", "x"))):
        own, succ, prev = others[colour::2]
        low, high = across[2 * colour : 2 * colour + 2]
        line = far_reduce(own, succ, low, high, prev, far)
        sums.append(near_reduce(line[0], line[1], line[2], line[3], near))
    column = jnp.concatenate(sums, axis=1).reshape(n_z, -1, half)
    column = lax.all_to_all(column, "z", split_axis=0, concat_axis=0, tiled=True)
    total = added(*[column[k] for k in range(n_z)])

    mine = by_core(core, total[:tok_rows], total[tok_rows:])
    theirs = by_core(core, total[tok_rows:], total[:tok_rows])
    other = shift(theirs, "c", 1)
    return by_core(
        core, jnp.concatenate([mine, other], axis=1), jnp.concatenate([other, mine], axis=1)
    )


def solution(mesh):
    grid = Mesh(mesh.devices.reshape(8, 4, 4, 2), ("z", "y", "x", "c"))
    every = ("z", "y", "x", "c")
    plane = ("y", "x", "c")
    return jax.shard_map(
        step,
        mesh=grid,
        in_specs=(
            P(every, None),
            P(every, None),
            P(every, None),
            P(plane, None, "z"),
            P(plane, None, "z"),
            P(plane, "z", None),
        ),
        out_specs=P(every, None),
        check_vma=False,
    )
```

profile of v0, /device:TPU:1, one launch (start us, length us, event | category | flops | bytes accessed | tf_op | source)
XLA Modules:
  0.0 225.5 jit_solution(17074977856896762028)
XLA Ops:
  1.7 3.2 %collective-permute-start = (bf16[4,3712]{1,0:T(4,128)(2,1)S(1)}, bf16[4,3712]{1,0:T(4,128)(2,1)S(1)}, u32[]{:S(2)}, u32[]{:S(2)}) collective-permute-start(bf16[4,3712]{1,0:T(4,128)(2,1)S(1)} %concatenate.38), channel_id=1, source_target_pairs={{0,1},{1,0},{2,3},{3,2},{4,5},{5,4},{6,7},{7,6},{8,9},{9,8},{10,11... | collective-permute-start | bytes 89096 | tf_op jit(solution)/shard_map/ppermute | solution.py:16
  5.9 21.9 %all_to_all.10 = bf16[8,8,3712]{2,1,0:T(8,128)(2,1)S(1)} all-to-all(bf16[8,8,3712]{2,1,0:T(8,128)(2,1)S(1)} %broadcast_in_dim.24), channel_id=1, replica_groups=mesh['z'=8,'y'=4,'x'=4,'c'=2] {'z'}, dimensions={0} | all-to-all | bytes 950272 | tf_op jit(solution)/shard_map/all_to_all | solution.py:280
  27.9 3.0 %collective-permute-start.9 = (bf16[64,1792]{1,0:T(8,128)(2,1)S(1)}, bf16[64,1792]{1,0:T(8,128)(2,1)S(1)}, u32[]{:S(2)}, u32[]{:S(2)}) collective-permute-start(bf16[64,1792]{1,0:T(8,128)(2,1)S(1)} %get-tuple-element.32), channel_id=1, source_target_pairs={{0,16},{8,24},{16,0},{24,8},{1,17},{9,25},{17,1},{25,9},{2,18},{10... | collective-permute-start | bytes 688136 | tf_op jit(solution)/shard_map/ppermute | solution.py:16
  32.4 2.8 %collective-permute-start.2 = (bf16[64,1920]{1,0:T(8,128)(2,1)S(1)}, bf16[64,1920]{1,0:T(8,128)(2,1)S(1)}, u32[]{:S(2)}, u32[]{:S(2)}) collective-permute-start(bf16[64,1920]{1,0:T(8,128)(2,1)S(1)} %get-tuple-element.34), channel_id=1, source_target_pairs={{0,4},{2,6},{4,0},{6,2},{1,5},{3,7},{5,1},{7,3},{8,12},{10,14},{12... | collective-permute-start | bytes 737288 | tf_op jit(solution)/shard_map/ppermute | solution.py:16
  36.7 4.4 %collective-permute-done.8 = bf16[64,1792]{1,0:T(8,128)(2,1)S(1)} collective-permute-done((bf16[64,1792]{1,0:T(8,128)(2,1)S(1)}, bf16[64,1792]{1,0:T(8,128)(2,1)S(1)}, u32[]{:S(2)}, u32[]{:S(2)}) %collective-permute-start.8) | collective-permute-done | bytes 229408 | tf_op jit(solution)/shard_map/ppermute | solution.py:16
  42.5 2.8 %collective-permute-done.1 = bf16[64,1920]{1,0:T(8,128)(2,1)S(1)} collective-permute-done((bf16[64,1920]{1,0:T(8,128)(2,1)S(1)}, bf16[64,1920]{1,0:T(8,128)(2,1)S(1)}, u32[]{:S(2)}, u32[]{:S(2)}) %collective-permute-start.1) | collective-permute-done | bytes 245792 | tf_op jit(solution)/shard_map/ppermute | solution.py:16
  45.9 2.7 %collective-permute-start.4 = (bf16[4,64,1920]{2,1,0:T(8,128)(2,1)S(1)}, bf16[4,64,1920]{2,1,0:T(8,128)(2,1)}, u32[]{:S(2)}, u32[]{:S(2)}) collective-permute-start(bf16[4,64,1920]{2,1,0:T(8,128)(2,1)S(1)} %pad_maximum_fusion.refs_0_), channel_id=1, source_target_pairs={{0,24},{8,0},{16,8},{24,16},{1,25},{9,1},{17,9},{25,17},{2,26},{10... | collective-permute-start | bytes 2949128 | tf_op jit(solution)/shard_map/ppermute | solution.py:16
  48.6 5.0 %collective-permute-start.15 = (bf16[4,64,1920]{2,1,0:T(8,128)(2,1)S(1)}, bf16[4,64,1920]{2,1,0:T(8,128)(2,1)S(1)}, u32[]{:S(2)}, u32[]{:S(2)}) collective-permute-start(bf16[4,64,1920]{2,1,0:T(8,128)(2,1)S(1)} %pad_maximum_fusion.refs_0_), channel_id=1, source_target_pairs={{0,1},{1,0},{2,3},{3,2},{4,5},{5,4},{6,7},{7,6},{8,9},{9,8},{10,11... | collective-permute-start | bytes 2949128 | tf_op jit(solution)/shard_map/ppermute | solution.py:16
  53.6 11.7 %collective-permute-done.12.refs_9_ = bf16[4,64,1792]{2,1,0:T(8,128)(2,1)S(1)} collective-permute-done((bf16[4,64,1792]{2,1,0:T(8,128)(2,1)S(1)}, bf16[4,64,1792]{2,1,0:T(8,128)(2,1)S(1)}, u32[]{:S(2)}, u32[]{:S(2)}) %collective-permute-start.12) | collective-permute-done | bytes 917536 | tf_op jit(solution)/shard_map/ppermute | solution.py:16
  65.4 2.4 %collective-permute-start.20 = (bf16[4,64,1792]{2,1,0:T(8,128)(2,1)S(1)}, bf16[4,64,1792]{2,1,0:T(8,128)(2,1)S(1)}, u32[]{:S(2)}, u32[]{:S(2)}) collective-permute-start(bf16[4,64,1792]{2,1,0:T(8,128)(2,1)S(1)} %pad_maximum_fusion.1.refs_5_), channel_id=1, source_target_pairs={{0,1},{1,0},{2,3},{3,2},{4,5},{5,4},{6,7},{7,6},{8,9},{9,8},{10,11... | collective-permute-start | bytes 2752520 | tf_op jit(solution)/shard_map/ppermute | solution.py:16
  68.7 7.5 %collective-permute-done.11.refs_6_ = bf16[4,64,1792]{2,1,0:T(8,128)(2,1)} collective-permute-done((bf16[4,64,1792]{2,1,0:T(8,128)(2,1)S(1)}, bf16[4,64,1792]{2,1,0:T(8,128)(2,1)}, u32[]{:S(2)}, u32[]{:S(2)}) %collective-permute-start.11) | collective-permute-done | bytes 917536 | tf_op jit(solution)/shard_map/ppermute | solution.py:16
  78.3 2.8 %collective-permute-start.7 = (bf16[2,64,1920]{2,1,0:T(8,128)(2,1)S(1)}, bf16[2,64,1920]{2,1,0:T(8,128)(2,1)}, u32[]{:S(2)}, u32[]{:S(2)}) collective-permute-start(bf16[2,64,1920]{2,1,0:T(8,128)(2,1)S(1)} %slice.142), channel_id=1, source_target_pairs={{0,24},{8,0},{16,8},{24,16},{1,25},{9,1},{17,9},{25,17},{2,26},{10... | collective-permute-start | bytes 1474568 | tf_op jit(solution)/shard_map/ppermute | solution.py:16
  83.7 1.6 collective-permute-start.24
  86.2 6.8 %collective-permute-done.14.refs_8_ = bf16[2,64,1792]{2,1,0:T(8,128)(2,1)S(1)} collective-permute-done((bf16[2,64,1792]{2,1,0:T(8,128)(2,1)S(1)}, bf16[2,64,1792]{2,1,0:T(8,128)(2,1)S(1)}, u32[]{:S(2)}, u32[]{:S(2)}) %collective-permute-start.14) | collective-permute-done | bytes 458784 | tf_op jit(solution)/shard_map/ppermute | solution.py:16
  93.0 2.0 collective-permute-start.19
  111.0 15.4 %hidden.1.h_ref = bf16[2,4,4,64,256]{4,3,2,1,0:T(8,128)(2,1)} custom-call(s32[2]{0:T(128)S(1)} %pad_add_fusion.place_ref, bf16[4,64,1920]{2,1,0:T(8,128)(2,1)S(1)} %pad_maximum_fusion.refs_0_, bf16[4,64,1920]{2,1,0:T(8,128)(2,1)} %collective-permute-done.4.refs_1_, bf16[2,64,1920]{2,1,0:T(8,128)(2,1)S(1)} %collective-permute-done.6.refs_2_, ...), custom_call_target="tpu_custom_call" | custom-call | flops 7516192768 | bytes 25165824 | tf_op jit(solution)/shard_map/hidden/pallas_call | solution.py:127
  127.7 4.9 %down_send.2 = bf16[3,2,4,64,1792]{4,3,2,1,0:T(8,128)(2,1)S(1)} custom-call(s32[2]{0:T(128)S(1)} %pad_add_fusion.place_ref, bf16[2,4,4,64,256]{4,3,2,1,0:T(8,128)(2,1)S(1)} %copy-done.1, bf16[256,7168]{1,0:T(8,128)(2,1)S(1)} %bitcast.44), custom_call_target="tpu_custom_call" | custom-call | flops 1409286144 | bytes 5505024 | tf_op jit(solution)/shard_map/down_send/pallas_call | solution.py:229
  133.1 2.1 down_send.3
  135.4 9.0 %collective-permute-done.26.refs_0_ = bf16[1,2,4,64,1792]{4,3,2,1,0:T(8,128)(2,1)S(1)} collective-permute-done((bf16[1,2,4,64,1792]{4,3,2,1,0:T(8,128)(2,1)S(1)}, bf16[1,2,4,64,1792]{4,3,2,1,0:T(8,128)(2,1)S(1)}, u32[]{:S(2)}, u32[]{:S(2)}) %collective-permute-start.26) | collective-permute-done | bytes 1835040 | tf_op jit(solution)/shard_map/ppermute | solution.py:16
  144.4 3.2 %down_add.3 = (bf16[2,64,1792]{2,1,0:T(8,128)(2,1)S(1)}, bf16[2,64,1792]{2,1,0:T(8,128)(2,1)S(1)}, bf16[2,64,1792]{2,1,0:T(8,128)(2,1)S(1)}, bf16[2,64,1792]{2,1,0:T(8,128)(2,1)S(1)}) custom-call(s32[2]{0:T(128)S(1)} %pad_add_fusion.place_ref, bf16[2,4,4,64,256]{4,3,2,1,0:T(8,128)(2,1)S(1)} %copy-done.1, bf16[256,7168]{1,0:T(8,128)(2,1)S(1)} %bitcast.46, ...), custom_call_target="tpu_custom_call" | custom-call | flops 469762048 | bytes 3670016 | tf_op jit(solution)/shard_map/down_add/pallas_call | solution.py:229
  147.6 2.1 collective-permute-start.36
  149.6 2.7 %collective-permute-start.29 = (bf16[2,64,1792]{2,1,0:T(8,128)(2,1)S(1)}, bf16[2,64,1792]{2,1,0:T(8,128)(2,1)S(1)}, u32[]{:S(2)}, u32[]{:S(2)}) collective-permute-start(bf16[2,64,1792]{2,1,0:T(8,128)(2,1)S(1)} %get-tuple-element.19), channel_id=1, source_target_pairs={{0,24},{8,0},{16,8},{24,16},{1,25},{9,1},{17,9},{25,17},{2,26},{10... | collective-permute-start | bytes 1376264 | tf_op jit(solution)/shard_map/ppermute | solution.py:16
  152.3 6.3 %down_add.2 = (bf16[4,64,1792]{2,1,0:T(8,128)(2,1)S(1)}, bf16[4,64,1792]{2,1,0:T(8,128)(2,1)S(1)}, bf16[4,64,1792]{2,1,0:T(8,128)(2,1)S(1)}, bf16[4,64,1792]{2,1...) custom-call(s32[2]{0:T(128)S(1)} %pad_add_fusion.place_ref, ...), custom_call_target="tpu_custom_call" | custom-call | flops 1409286144 | bytes 11010048 | tf_op jit(solution)/shard_map/down_add/pallas_call | solution.py:229
  159.6 3.3 %collective-permute-start.37 = (bf16[4,64,1792]{2,1,0:T(8,128)(2,1)S(1)}, bf16[4,64,1792]{2,1,0:T(8,128)(2,1)S(1)}, u32[]{:S(2)}, u32[]{:S(2)}) collective-permute-start(bf16[4,64,1792]{2,1,0:T(8,128)(2,1)S(1)} %pad_maximum_fusion.5), channel_id=1, source_target_pairs={{0,6},{2,0},{4,2},{6,4},{1,7},{3,1},{5,3},{7,5},{8,14},{10,8},{12,... | collective-permute-start | bytes 2752520 | tf_op jit(solution)/shard_map/ppermute | solution.py:16
  166.8 14.6 %collective-permute-done.37 = bf16[4,64,1792]{2,1,0:T(8,128)(2,1)S(1)} collective-permute-done((bf16[4,64,1792]{2,1,0:T(8,128)(2,1)S(1)}, bf16[4,64,1792]{2,1,0:T(8,128)(2,1)S(1)}, u32[]{:S(2)}, u32[]{:S(2)}) %collective-permute-start.37) | collective-permute-done | bytes 917536 | tf_op jit(solution)/shard_map/ppermute | solution.py:16
  181.4 4.4 %collective-permute-done.35 = bf16[4,64,1792]{2,1,0:T(8,128)(2,1)S(1)} collective-permute-done((bf16[4,64,1792]{2,1,0:T(8,128)(2,1)S(1)}, bf16[4,64,1792]{2,1,0:T(8,128)(2,1)S(1)}, u32[]{:S(2)}, u32[]{:S(2)}) %collective-permute-start.35) | collective-permute-done | bytes 917536 | tf_op jit(solution)/shard_map/ppermute | solution.py:16
  186.2 2.7 %collective-permute-start.40 = (bf16[64,1792]{1,0:T(8,128)(2,1)S(1)}, bf16[64,1792]{1,0:T(8,128)(2,1)S(1)}, u32[]{:S(2)}, u32[]{:S(2)}) collective-permute-start(bf16[64,1792]{1,0:T(8,128)(2,1)S(1)} %get-tuple-element.29), channel_id=1, source_target_pairs={{0,24},{8,0},{16,8},{24,16},{1,25},{9,1},{17,9},{25,17},{2,26},{10... | collective-permute-start | bytes 688136 | tf_op jit(solution)/shard_map/ppermute | solution.py:16
  189.4 2.7 %collective-permute-start.33 = (bf16[64,1792]{1,0:T(8,128)(2,1)S(1)}, bf16[64,1792]{1,0:T(8,128)(2,1)S(1)}, u32[]{:S(2)}, u32[]{:S(2)}) collective-permute-start(bf16[64,1792]{1,0:T(8,128)(2,1)S(1)} %get-tuple-element.26), channel_id=1, source_target_pairs={{0,6},{2,0},{4,2},{6,4},{1,7},{3,1},{5,3},{7,5},{8,14},{10,8},{12,... | collective-permute-start | bytes 688136 | tf_op jit(solution)/shard_map/ppermute | solution.py:16
  194.7 2.7 %collective-permute-done.39 = bf16[64,1792]{1,0:T(8,128)(2,1)S(1)} collective-permute-done((bf16[64,1792]{1,0:T(8,128)(2,1)S(1)}, bf16[64,1792]{1,0:T(8,128)(2,1)S(1)}, u32[]{:S(2)}, u32[]{:S(2)}) %collective-permute-start.39) | collective-permute-done | bytes 229408 | tf_op jit(solution)/shard_map/ppermute | solution.py:16
  197.6 1.5 collective-permute-done.32
  199.3 13.8 %all_to_all.11 = bf16[8,8,3584]{2,1,0:T(8,128)(2,1)S(1)} all-to-all(bf16[8,8,3584]{2,1,0:T(8,128)(2,1)S(1)} %maximum_bitcast_fusion), channel_id=1, replica_groups=mesh['z'=8,'y'=4,'x'=4,'c'=2] {'z'}, dimensions={0} | all-to-all | bytes 917504 | tf_op jit(solution)/shard_map/all_to_all | solution.py:304
  213.2 10.8 %collective-permute-start.41 = (bf16[4,3584]{1,0:T(4,128)(2,1)S(1)}, bf16[4,3584]{1,0:T(4,128)(2,1)S(1)}, u32[]{:S(2)}, u32[]{:S(2)}) collective-permute-start(bf16[4,3584]{1,0:T(4,128)(2,1)S(1)} %get-tuple-element.36), channel_id=1, source_target_pairs={{0,1},{1,0},{2,3},{3,2},{4,5},{5,4},{6,7},{7,6},{8,9},{9,8},{10,11... | collective-permute-start | bytes 86024 | tf_op jit(solution)/shard_map/ppermute | solution.py:16
  (134 shorter events, 42.4 us)
Async XLA Ops:
  30.9 10.2 %collective-permute-start.8 = (bf16[64,1792]{1,0:T(8,128)(2,1)S(1)}, bf16[64,1792]{1,0:T(8,128)(2,1)S(1)}, u32[]{:S(2)}, u32[]{:S(2)}) collective-permute-start(bf16[64,1792]{1,0:T(8,128)(2,1)S(1)} %get-tuple-element.32), channel_id=1, source_target_pairs={{0,24},{8,0},{16,8},{24,16},{1,25},{9,1},{17,9},{25,17},{2,26},{10... | collective-permute-start | bytes 688136 | tf_op jit(solution)/shard_map/ppermute | solution.py:16
  31.6 9.4 %collective-permute-start.10 = (bf16[64,1792]{1,0:T(8,128)(2,1)S(1)}, bf16[64,1792]{1,0:T(8,128)(2,1)S(1)}, u32[]{:S(2)}, u32[]{:S(2)}) collective-permute-start(bf16[64,1792]{1,0:T(8,128)(2,1)S(1)} %get-tuple-element.32), channel_id=1, source_target_pairs={{0,8},{8,16},{16,24},{24,0},{1,9},{9,17},{17,25},{25,1},{2,10},{10... | collective-permute-start | bytes 688136 | tf_op jit(solution)/shard_map/ppermute | solution.py:16
  32.4 10.1 %collective-permute-start.2 = (bf16[64,1920]{1,0:T(8,128)(2,1)S(1)}, bf16[64,1920]{1,0:T(8,128)(2,1)S(1)}, u32[]{:S(2)}, u32[]{:S(2)}) collective-permute-start(bf16[64,1920]{1,0:T(8,128)(2,1)S(1)} %get-tuple-element.34), channel_id=1, source_target_pairs={{0,4},{2,6},{4,0},{6,2},{1,5},{3,7},{5,1},{7,3},{8,12},{10,14},{12... | collective-permute-start | bytes 737288 | tf_op jit(solution)/shard_map/ppermute | solution.py:16
  35.2 10.1 %collective-permute-start.1 = (bf16[64,1920]{1,0:T(8,128)(2,1)S(1)}, bf16[64,1920]{1,0:T(8,128)(2,1)S(1)}, u32[]{:S(2)}, u32[]{:S(2)}) collective-permute-start(bf16[64,1920]{1,0:T(8,128)(2,1)S(1)} %get-tuple-element.34), channel_id=1, source_target_pairs={{0,6},{2,0},{4,2},{6,4},{1,7},{3,1},{5,3},{7,5},{8,14},{10,8},{12,... | collective-permute-start | bytes 737288 | tf_op jit(solution)/shard_map/ppermute | solution.py:16
  36.1 9.6 %collective-permute-start.3 = (bf16[64,1920]{1,0:T(8,128)(2,1)S(1)}, bf16[64,1920]{1,0:T(8,128)(2,1)S(1)}, u32[]{:S(2)}, u32[]{:S(2)}) collective-permute-start(bf16[64,1920]{1,0:T(8,128)(2,1)S(1)} %get-tuple-element.34), channel_id=1, source_target_pairs={{0,2},{2,4},{4,6},{6,0},{1,3},{3,5},{5,7},{7,1},{8,10},{10,12},{12... | collective-permute-start | bytes 737288 | tf_op jit(solution)/shard_map/ppermute | solution.py:16
  41.2 24.1 %collective-permute-start.12 = (bf16[4,64,1792]{2,1,0:T(8,128)(2,1)S(1)}, bf16[4,64,1792]{2,1,0:T(8,128)(2,1)S(1)}, u32[]{:S(2)}, u32[]{:S(2)}) collective-permute-start(bf16[4,64,1792]{2,1,0:T(8,128)(2,1)S(1)} %pad_maximum_fusion.1.refs_5_), channel_id=1, source_target_pairs={{0,2},{2,4},{4,6},{6,0},{1,3},{3,5},{5,7},{7,1},{8,10},{10,12},{12... | collective-permute-start | bytes 2752520 | tf_op jit(solution)/shard_map/ppermute | solution.py:16
  45.8 22.0 %collective-permute-start.5 = (bf16[4,64,1920]{2,1,0:T(8,128)(2,1)S(1)}, bf16[4,64,1920]{2,1,0:T(8,128)(2,1)S(1)}, u32[]{:S(2)}, u32[]{:S(2)}) collective-permute-start(bf16[4,64,1920]{2,1,0:T(8,128)(2,1)S(1)} %pad_maximum_fusion.refs_0_), channel_id=1, source_target_pairs={{0,8},{8,16},{16,24},{24,0},{1,9},{9,17},{17,25},{25,1},{2,10},{10... | collective-permute-start | bytes 2949128 | tf_op jit(solution)/shard_map/ppermute | solution.py:16
  45.9 31.3 %collective-permute-start.4 = (bf16[4,64,1920]{2,1,0:T(8,128)(2,1)S(1)}, bf16[4,64,1920]{2,1,0:T(8,128)(2,1)}, u32[]{:S(2)}, u32[]{:S(2)}) collective-permute-start(bf16[4,64,1920]{2,1,0:T(8,128)(2,1)S(1)} %pad_maximum_fusion.refs_0_), channel_id=1, source_target_pairs={{0,24},{8,0},{16,8},{24,16},{1,25},{9,1},{17,9},{25,17},{2,26},{10... | collective-permute-start | bytes 2949128 | tf_op jit(solution)/shard_map/ppermute | solution.py:16
  48.6 34.2 %collective-permute-start.15 = (bf16[4,64,1920]{2,1,0:T(8,128)(2,1)S(1)}, bf16[4,64,1920]{2,1,0:T(8,128)(2,1)S(1)}, u32[]{:S(2)}, u32[]{:S(2)}) collective-permute-start(bf16[4,64,1920]{2,1,0:T(8,128)(2,1)S(1)} %pad_maximum_fusion.refs_0_), channel_id=1, source_target_pairs={{0,1},{1,0},{2,3},{3,2},{4,5},{5,4},{6,7},{7,6},{8,9},{9,8},{10,11... | collective-permute-start | bytes 2949128 | tf_op jit(solution)/shard_map/ppermute | solution.py:16
  53.6 22.5 %collective-permute-start.11 = (bf16[4,64,1792]{2,1,0:T(8,128)(2,1)S(1)}, bf16[4,64,1792]{2,1,0:T(8,128)(2,1)}, u32[]{:S(2)}, u32[]{:S(2)}) collective-permute-start(bf16[4,64,1792]{2,1,0:T(8,128)(2,1)S(1)} %pad_maximum_fusion.1.refs_5_), channel_id=1, source_target_pairs={{0,6},{2,0},{4,2},{6,4},{1,7},{3,1},{5,3},{7,5},{8,14},{10,8},{12,... | collective-permute-start | bytes 2752520 | tf_op jit(solution)/shard_map/ppermute | solution.py:16
  65.4 15.7 %collective-permute-start.20 = (bf16[4,64,1792]{2,1,0:T(8,128)(2,1)S(1)}, bf16[4,64,1792]{2,1,0:T(8,128)(2,1)S(1)}, u32[]{:S(2)}, u32[]{:S(2)}) collective-permute-start(bf16[4,64,1792]{2,1,0:T(8,128)(2,1)S(1)} %pad_maximum_fusion.1.refs_5_), channel_id=1, source_target_pairs={{0,1},{1,0},{2,3},{3,2},{4,5},{5,4},{6,7},{7,6},{8,9},{9,8},{10,11... | collective-permute-start | bytes 2752520 | tf_op jit(solution)/shard_map/ppermute | solution.py:16
  67.8 17.5 %collective-permute-start.13 = (bf16[2,64,1792]{2,1,0:T(8,128)(2,1)S(1)}, bf16[2,64,1792]{2,1,0:T(8,128)(2,1)S(1)}, u32[]{:S(2)}, u32[]{:S(2)}) collective-permute-start(bf16[2,64,1792]{2,1,0:T(8,128)(2,1)S(1)} %slice.144), channel_id=1, source_target_pairs={{0,2},{2,4},{4,6},{6,0},{1,3},{3,5},{5,7},{7,1},{8,10},{10,12},{12... | collective-permute-start | bytes 1376264 | tf_op jit(solution)/shard_map/ppermute | solution.py:16
  76.2 18.8 %collective-permute-start.6 = (bf16[2,64,1920]{2,1,0:T(8,128)(2,1)S(1)}, bf16[2,64,1920]{2,1,0:T(8,128)(2,1)S(1)}, u32[]{:S(2)}, u32[]{:S(2)}) collective-permute-start(bf16[2,64,1920]{2,1,0:T(8,128)(2,1)S(1)} %slice.141), channel_id=1, source_target_pairs={{0,8},{8,16},{16,24},{24,0},{1,9},{9,17},{17,25},{25,1},{2,10},{10... | collective-permute-start | bytes 1474568 | tf_op jit(solution)/shard_map/ppermute | solution.py:16
  78.3 16.7 %collective-permute-start.7 = (bf16[2,64,1920]{2,1,0:T(8,128)(2,1)S(1)}, bf16[2,64,1920]{2,1,0:T(8,128)(2,1)}, u32[]{:S(2)}, u32[]{:S(2)}) collective-permute-start(bf16[2,64,1920]{2,1,0:T(8,128)(2,1)S(1)} %slice.142), channel_id=1, source_target_pairs={{0,24},{8,0},{16,8},{24,16},{1,25},{9,1},{17,9},{25,17},{2,26},{10... | collective-permute-start | bytes 1474568 | tf_op jit(solution)/shard_map/ppermute | solution.py:16
  82.0 10.9 %collective-permute-start.14 = (bf16[2,64,1792]{2,1,0:T(8,128)(2,1)S(1)}, bf16[2,64,1792]{2,1,0:T(8,128)(2,1)S(1)}, u32[]{:S(2)}, u32[]{:S(2)}) collective-permute-start(bf16[2,64,1792]{2,1,0:T(8,128)(2,1)S(1)} %slice.145), channel_id=1, source_target_pairs={{0,6},{2,0},{4,2},{6,4},{1,7},{3,1},{5,3},{7,5},{8,14},{10,8},{12,... | collective-permute-start | bytes 1376264 | tf_op jit(solution)/shard_map/ppermute | solution.py:16
  83.7 13.4 %collective-permute-start.24 = (bf16[4,64,1792]{2,1,0:T(8,128)(2,1)S(1)}, bf16[4,64,1792]{2,1,0:T(8,128)(2,1)S(1)}, u32[]{:S(2)}, u32[]{:S(2)}) collective-permute-start(bf16[4,64,1792]{2,1,0:T(8,128)(2,1)S(1)} %collective-permute-done.12.refs_9_), channel_id=1, source_target_pairs={{0,1},{1,0},{2,3},{3,2},{4,5},{5,4},{6,7},{7,6},{8,9},{9,8},{10,11... | collective-permute-start | bytes 2752520 | tf_op jit(solution)/shard_map/ppermute | solution.py:16
  85.4 10.9 %collective-permute-start.22 = (bf16[2,64,1792]{2,1,0:T(8,128)(2,1)S(1)}, bf16[2,64,1792]{2,1,0:T(8,128)(2,1)S(1)}, u32[]{:S(2)}, u32[]{:S(2)}) collective-permute-start(bf16[2,64,1792]{2,1,0:T(8,128)(2,1)S(1)} %collective-permute-done.13.refs_7_), channel_id=1, source_target_pairs={{0,1},{1,0},{2,3},{3,2},{4,5},{5,4},{6,7},{7,6},{8,9},{9,8},{10,11... | collective-permute-start | bytes 1376264 | tf_op jit(solution)/shard_map/ppermute | solution.py:16
  93.0 8.4 %collective-permute-start.19 = (bf16[4,64,1920]{2,1,0:T(8,128)(2,1)S(1)}, bf16[4,64,1920]{2,1,0:T(8,128)(2,1)}, u32[]{:S(2)}, u32[]{:S(2)}) collective-permute-start(bf16[4,64,1920]{2,1,0:T(8,128)(2,1)S(1)} %collective-permute-done.5.refs_4_), channel_id=1, source_target_pairs={{0,1},{1,0},{2,3},{3,2},{4,5},{5,4},{6,7},{7,6},{8,9},{9,8},{10,11... | collective-permute-start | bytes 2949128 | tf_op jit(solution)/shard_map/ppermute | solution.py:16
  132.6 19.7 %collective-permute-start.25 = (bf16[3,2,4,64,1792]{4,3,2,1,0:T(8,128)(2,1)S(1)}, bf16[3,2,4,64,1792]{4,3,2,1,0:T(8,128)(2,1)S(1)}, u32[]{:S(2)}, u32[]{:S(2)}) collective-permute-start(bf16[3,2,4,64,1792]{4,3,2,1,0:T(8,128)(2,1)S(1)} %down_send.2), channel_id=1, source_target_pairs={{0,1},{1,0},{2,3},{3,2},{4,5},{5,4},{6,7},{7,6},{8,9},{9,8},{10,11... | collective-permute-start | bytes 16515080 | tf_op jit(solution)/shard_map/ppermute | solution.py:16
  135.2 9.2 %collective-permute-start.26 = (bf16[1,2,4,64,1792]{4,3,2,1,0:T(8,128)(2,1)S(1)}, bf16[1,2,4,64,1792]{4,3,2,1,0:T(8,128)(2,1)S(1)}, u32[]{:S(2)}, u32[]{:S(2)}) collective-permute-start(bf16[1,2,4,64,1792]{4,3,2,1,0:T(8,128)(2,1)S(1)} %down_send.3), channel_id=1, source_target_pairs={{0,1},{1,0},{2,3},{3,2},{4,5},{5,4},{6,7},{7,6},{8,9},{9,8},{10,11... | collective-permute-start | bytes 5505032 | tf_op jit(solution)/shard_map/ppermute | solution.py:16
  147.6 11.8 %collective-permute-start.36 = (bf16[2,64,1792]{2,1,0:T(8,128)(2,1)S(1)}, bf16[2,64,1792]{2,1,0:T(8,128)(2,1)S(1)}, u32[]{:S(2)}, u32[]{:S(2)}) collective-permute-start(bf16[2,64,1792]{2,1,0:T(8,128)(2,1)S(1)} %get-tuple-element.24), channel_id=1, source_target_pairs={{0,6},{2,0},{4,2},{6,4},{1,7},{3,1},{5,3},{7,5},{8,14},{10,8},{12,... | collective-permute-start | bytes 1376264 | tf_op jit(solution)/shard_map/ppermute | solution.py:16
  149.6 15.7 %collective-permute-start.27 = (bf16[2,64,1792]{2,1,0:T(8,128)(2,1)S(1)}, bf16[2,64,1792]{2,1,0:T(8,128)(2,1)S(1)}, u32[]{:S(2)}, u32[]{:S(2)}) collective-permute-start(bf16[2,64,1792]{2,1,0:T(8,128)(2,1)S(1)} %get-tuple-element.17), channel_id=1, source_target_pairs={{0,8},{8,16},{16,24},{24,0},{1,9},{9,17},{17,25},{25,1},{2,10},{10... | collective-permute-start | bytes 1376264 | tf_op jit(solution)/shard_map/ppermute | solution.py:16
  149.6 15.1 %collective-permute-start.29 = (bf16[2,64,1792]{2,1,0:T(8,128)(2,1)S(1)}, bf16[2,64,1792]{2,1,0:T(8,128)(2,1)S(1)}, u32[]{:S(2)}, u32[]{:S(2)}) collective-permute-start(bf16[2,64,1792]{2,1,0:T(8,128)(2,1)S(1)} %get-tuple-element.19), channel_id=1, source_target_pairs={{0,24},{8,0},{16,8},{24,16},{1,25},{9,1},{17,9},{25,17},{2,26},{10... | collective-permute-start | bytes 1376264 | tf_op jit(solution)/shard_map/ppermute | solution.py:16
  152.3 12.1 %collective-permute-start.34 = (bf16[2,64,1792]{2,1,0:T(8,128)(2,1)S(1)}, bf16[2,64,1792]{2,1,0:T(8,128)(2,1)S(1)}, u32[]{:S(2)}, u32[]{:S(2)}) collective-permute-start(bf16[2,64,1792]{2,1,0:T(8,128)(2,1)S(1)} %get-tuple-element.22), channel_id=1, source_target_pairs={{0,2},{2,4},{4,6},{6,0},{1,3},{3,5},{5,7},{7,1},{8,10},{10,12},{12... | collective-permute-start | bytes 1376264 | tf_op jit(solution)/shard_map/ppermute | solution.py:16
  159.6 21.7 %collective-permute-start.37 = (bf16[4,64,1792]{2,1,0:T(8,128)(2,1)S(1)}, bf16[4,64,1792]{2,1,0:T(8,128)(2,1)S(1)}, u32[]{:S(2)}, u32[]{:S(2)}) collective-permute-start(bf16[4,64,1792]{2,1,0:T(8,128)(2,1)S(1)} %pad_maximum_fusion.5), channel_id=1, source_target_pairs={{0,6},{2,0},{4,2},{6,4},{1,7},{3,1},{5,3},{7,5},{8,14},{10,8},{12,... | collective-permute-start | bytes 2752520 | tf_op jit(solution)/shard_map/ppermute | solution.py:16
  164.6 21.1 %collective-permute-start.35 = (bf16[4,64,1792]{2,1,0:T(8,128)(2,1)S(1)}, bf16[4,64,1792]{2,1,0:T(8,128)(2,1)S(1)}, u32[]{:S(2)}, u32[]{:S(2)}) collective-permute-start(bf16[4,64,1792]{2,1,0:T(8,128)(2,1)S(1)} %pad_maximum_fusion.4), channel_id=1, source_target_pairs={{0,2},{2,4},{4,6},{6,0},{1,3},{3,5},{5,7},{7,1},{8,10},{10,12},{12... | collective-permute-start | bytes 2752520 | tf_op jit(solution)/shard_map/ppermute | solution.py:16
  165.0 23.9 %collective-permute-start.30 = (bf16[4,64,1792]{2,1,0:T(8,128)(2,1)S(1)}, bf16[4,64,1792]{2,1,0:T(8,128)(2,1)S(1)}, u32[]{:S(2)}, u32[]{:S(2)}) collective-permute-start(bf16[4,64,1792]{2,1,0:T(8,128)(2,1)S(1)} %pad_maximum_fusion.3), channel_id=1, source_target_pairs={{0,24},{8,0},{16,8},{24,16},{1,25},{9,1},{17,9},{25,17},{2,26},{10... | collective-permute-start | bytes 2752520 | tf_op jit(solution)/shard_map/ppermute | solution.py:16
  165.5 23.4 %collective-permute-start.28 = (bf16[4,64,1792]{2,1,0:T(8,128)(2,1)S(1)}, bf16[4,64,1792]{2,1,0:T(8,128)(2,1)S(1)}, u32[]{:S(2)}, u32[]{:S(2)}) collective-permute-start(bf16[4,64,1792]{2,1,0:T(8,128)(2,1)S(1)} %pad_maximum_fusion.2), channel_id=1, source_target_pairs={{0,8},{8,16},{16,24},{24,0},{1,9},{9,17},{17,25},{25,1},{2,10},{10... | collective-permute-start | bytes 2752520 | tf_op jit(solution)/shard_map/ppermute | solution.py:16
  186.2 8.5 %collective-permute-start.40 = (bf16[64,1792]{1,0:T(8,128)(2,1)S(1)}, bf16[64,1792]{1,0:T(8,128)(2,1)S(1)}, u32[]{:S(2)}, u32[]{:S(2)}) collective-permute-start(bf16[64,1792]{1,0:T(8,128)(2,1)S(1)} %get-tuple-element.29), channel_id=1, source_target_pairs={{0,24},{8,0},{16,8},{24,16},{1,25},{9,1},{17,9},{25,17},{2,26},{10... | collective-permute-start | bytes 688136 | tf_op jit(solution)/shard_map/ppermute | solution.py:16
  188.9 8.5 %collective-permute-start.39 = (bf16[64,1792]{1,0:T(8,128)(2,1)S(1)}, bf16[64,1792]{1,0:T(8,128)(2,1)S(1)}, u32[]{:S(2)}, u32[]{:S(2)}) collective-permute-start(bf16[64,1792]{1,0:T(8,128)(2,1)S(1)} %get-tuple-element.30), channel_id=1, source_target_pairs={{0,16},{8,24},{16,0},{24,8},{1,17},{9,25},{17,1},{25,9},{2,18},{10... | collective-permute-start | bytes 688136 | tf_op jit(solution)/shard_map/ppermute | solution.py:16
  189.3 8.3 %collective-permute-start.31 = (bf16[64,1792]{1,0:T(8,128)(2,1)S(1)}, bf16[64,1792]{1,0:T(8,128)(2,1)S(1)}, u32[]{:S(2)}, u32[]{:S(2)}) collective-permute-start(bf16[64,1792]{1,0:T(8,128)(2,1)S(1)} %get-tuple-element.25), channel_id=1, source_target_pairs={{0,2},{2,4},{4,6},{6,0},{1,3},{3,5},{5,7},{7,1},{8,10},{10,12},{12... | collective-permute-start | bytes 688136 | tf_op jit(solution)/shard_map/ppermute | solution.py:16
  213.2 11.6 %collective-permute-start.41 = (bf16[4,3584]{1,0:T(4,128)(2,1)S(1)}, bf16[4,3584]{1,0:T(4,128)(2,1)S(1)}, u32[]{:S(2)}, u32[]{:S(2)}) collective-permute-start(bf16[4,3584]{1,0:T(4,128)(2,1)S(1)} %get-tuple-element.36), channel_id=1, source_target_pairs={{0,1},{1,0},{2,3},{3,2},{4,5},{5,4},{6,7},{7,6},{8,9},{9,8},{10,11... | collective-permute-start | bytes 86024 | tf_op jit(solution)/shard_map/ppermute | solution.py:16
  (28 other events, 102.9 us)
where the time goes:
time: 226 us; the launch traced here: 225 us
  waiting for transfers between devices  73.3 us (32%)
  starting transfers between devices  60.9 us (27%)
  blocking collectives  35.8 us (16%)
  Pallas kernels  32 us (14%)
  local copies, waits for them, and re-layouts  18.8 us (8%)
  other arithmetic  4.45 us (2%)
    ppermute x42, waiting for transfers between devices, shift(): return lax.ppermute(value, axis, [(i, (i + step) % n) for i in range(n)])  73.3 us
    ppermute x42, starting transfers between devices, shift(): return lax.ppermute(value, axis, [(i, (i + step) % n) for i in range(n)])  60.9 us
    all_to_all x2, blocking collectives, step(): lax.all_to_all(column, 'z', split_axis=0, concat_axis=0, tiled=True)  35.8 us
    pallas_call x4, Pallas kernels, down_call(): pl.pallas_call(functools.partial(down_kernel, offsets, adds), out_shape=[...  16.5 us
    unnamed x36, local copies, waits for them, and re-layouts  16 us
    pallas_call x1, Pallas kernels, hidden_call(): pl.pallas_call(hidden_kernel, out_shape=jax.ShapeDtypeStruct((2, 4, 4, ro...  15.4 us
  transfers between devices with their start and end apart: 42, of which 21 were waited for; matrix products, arithmetic and copies ran while one was open for 2% of the time, Pallas kernels for 5%

commit v1 on v0

--- a/solution.py
+++ b/solution.py
@@ -17,7 +17,7 @@
 
 
 def near_gather(own, axis):
-    return jnp.stack([own, shift(own, axis, -1), shift(own, axis, 2), shift(own, axis, 1)])
+    return jnp.concatenate([own, shift(own, axis, -1), shift(own, axis, 2), shift(own, axis, 1)])
 
 
 def near_reduce(own, succ, across, prev, axis):
@@ -25,12 +25,15 @@
 
 
 def far_gather(own, axis):
+    n = lax.axis_size(axis)
     half = own.shape[0] // 2
-    prev = shift(own, axis, 1)
-    succ = shift(own, axis, -1)
-    low = shift(prev[:half], axis, 1)
-    high = shift(succ[half:], axis, -1)
-    return own, succ, low, high, prev
+    pieces = [(0, 0, own)]
+    prev = succ = own
+    for k in range(1, n // 2):
+        prev, succ = shift(prev, axis, 1), shift(succ, axis, -1)
+        pieces += [(k, 0, succ), (n - k, 0, prev)]
+    low, high = shift(prev[:half], axis, 1), shift(succ[half:], axis, -1)
+    return pieces + [(n // 2, 0, low), (n // 2, half, high)]
 
 
 def far_reduce(own, succ, low, high, prev, axis):
@@ -53,99 +56,135 @@
     return jnp.where(core == 0, if_zero, if_one)
 
 
-PLACES = ((0, 0, 4), (1, 0, 4), (2, 0, 2), (2, 2, 2), (3, 0, 4))
-
-
-def hidden_kernel(place_ref, *refs):
-    pieces, (gate_ref, up_ref, out_ref) = refs[:20], refs[20:23]
-    x_buf, w_buf, acc, named, x_sem, w_sem, named_sem = refs[23:]
-    rows, width = x_buf.shape[3:]
+def hidden_kernel(count, spots, place_ref, *refs):
+    sources, (gate_ref, up_ref, down_ref, out_ref, sent_ref) = refs[:count], refs[count : count + 5]
+    x_buf, w_buf, acc, named, d_buf, o_buf, x_sem, w_sem, named_sem, d_sem, o_sem = refs[count + 5 :]
+    lines, width = x_buf.shape[2:]
+    rows = lines // 4
     ff = gate_ref.shape[1]
     core, expert = place_ref[0], place_ref[1]
     for side in range(2):
-        which = core if side == 0 else 1 - core
-        half = pl.ds(pl.multiple_of(which * 2 * width, LANES), 2 * width)
-        for k, ref in enumerate((gate_ref, up_ref)):
+        half = core if side == 0 else 1 - core
+        for colour in range(2):
+            part = pl.ds(pl.multiple_of((2 * half + colour) * width, LANES), width)
+            for k, ref in enumerate((gate_ref, up_ref)):
+                pltpu.make_async_copy(
+                    ref.at[part, :],
+                    w_buf.at[2 * side + colour, :, k * ff : (k + 1) * ff],
+                    w_sem.at[2 * side + colour],
+                ).start()
+        for which, colour, first, source, begin, length in spots:
+            if which == side:
+                skip = sources[source].shape[1] - width
+                block, row = first // lines, first % lines
+                pltpu.make_async_copy(
+                    sources[source].at[begin : begin + length, skip : skip + width],
+                    x_buf.at[2 * side + colour, block, row : row + length],
+                    x_sem.at[2 * side + colour, block],
+                ).start()
+    for side, colour, first, source, begin, length in spots:
+        if side == 0 and colour == 0:
             pltpu.make_async_copy(
-                ref.at[half, :], w_buf.at[side, :, k * ff : (k + 1) * ff], w_sem.at[side]
+                sources[source].at[begin : begin + length, :LANES],
+                named.at[first // lines, first % lines : first % lines + length],
+                named_sem,
             ).start()
-        for i in range(side * 10, side * 10 + 10):
-            group = i // 5
-            offset, first, count = PLACES[i % 5]
-            skip = pieces[i].shape[2] - width
-            pltpu.make_async_copy(
-                pieces[i].at[:, :, skip : skip + width],
-                x_buf.at[group, offset, first : first + count],
-                x_sem.at[group, offset],
-            ).start()
-    for i, (offset, first, count) in enumerate(PLACES):
-        pltpu.make_async_copy(
-            pieces[i].at[:, :, :LANES], named.at[offset, first : first + count], named_sem
-        ).start()
+
+    for colour in range(2):
+        part = pl.ds(pl.multiple_of((2 * (1 - core) + colour) * width, LANES), width)
+        pltpu.make_async_copy(down_ref.at[:, part], d_buf.at[colour], d_sem.at[colour]).start()
 
     def step(i, _):
-        group, offset = i // 4, i % 4
+        group, pair = i // 2, i % 2
         side, colour = group // 2, group % 2
 
-        @pl.when(i % 8 == 0)
+        @pl.when(pair == 0)
         def _():
-            pltpu.make_async_copy(w_buf.at[side], w_buf.at[side], w_sem.at[side]).wait()
-
-        there = x_buf.at[group, offset]
-        pltpu.make_async_copy(there, there, x_sem.at[group, offset]).wait()
-        x = x_buf[group, offset].reshape(4 * rows, width)
-        w = w_buf[side, pl.ds(pl.multiple_of(colour * width, LANES), width), :]
-        part = jnp.dot(x, w, preferred_element_type=jnp.float32).reshape(4, rows, 2 * ff)
-        acc[colour, offset] = jnp.where(side == 0, part, part + acc[colour, offset])
+            pltpu.make_async_copy(w_buf.at[group], w_buf.at[group], w_sem.at[group]).wait()
+
+        for block in range(2):
+            there = x_buf.at[group, 2 * pair + block]
+            pltpu.make_async_copy(there, there, x_sem.at[group, 2 * pair + block]).wait()
+        x = x_buf[group, pl.ds(2 * pair, 2)].reshape(2 * lines, width)
+        part = jnp.dot(x, w_buf[group], preferred_element_type=jnp.float32)
+        at = pl.ds(pl.multiple_of(2 * pair * lines, 8), 2 * lines)
+        acc[colour, at, :] = jnp.where(side == 0, part, part + acc[colour, at, :])
         return 0
 
-    lax.fori_loop(0, 16, step, 0)
+    lax.fori_loop(0, 8, step, 0)
     pltpu.make_async_copy(named, named, named_sem).wait()
     lane = lax.broadcasted_iota(jnp.int32, (LANES, ff), 0)
     chosen = ((lane == expert) | (lane == expert + LANES // 2)).astype(jnp.bfloat16)
 
     def finish(offset, _):
-        weight = jnp.dot(
-            named[offset].reshape(4 * rows, LANES), chosen, preferred_element_type=jnp.float32
-        ).reshape(4, rows, ff)
+        weight = jnp.dot(named[offset], chosen, preferred_element_type=jnp.float32)
         for j in range(4):
-            gate = acc[0, offset, j, :, :ff] + acc[1, j, offset, :, :ff]
-            up = acc[0, offset, j, :, ff:] + acc[1, j, offset, :, ff:]
-            act = (gate / (1.0 + jnp.exp(-gate)) * up * weight[j]).astype(jnp.bfloat16)
+            theirs = pl.ds(pl.multiple_of(j * lines + offset * rows, 8), rows)
+            mine = pl.ds(pl.multiple_of(offset * lines + j * rows, 8), rows)
+            total = acc[0, mine, :] + acc[1, theirs, :]
+            gate, up = total[:, :ff], total[:, ff:]
+            act = gate / (1.0 + jnp.exp(-gate)) * up * weight[j * rows : (j + 1) * rows]
+            act = act.astype(jnp.bfloat16)
             out_ref[0, offset, j] = act
             out_ref[1, j, offset] = act
         return 0
 
     lax.fori_loop(0, 4, finish, 0)
 
-
-def hidden_call(place, own, sibling, gate_mat, up_mat):
-    rows = own[0].shape[1]
+    steps = 2 if width % (4 * LANES) == 0 else 1
+    tile = width // steps
+    for colour in range(2):
+        pltpu.make_async_copy(d_buf.at[colour], d_buf.at[colour], d_sem.at[colour]).wait()
+
+    def column(i, _):
+        colour = i // steps
+        at = pl.ds(pl.multiple_of(i % steps * tile, LANES), tile)
+        h = out_ref[colour, 2].reshape(lines, ff)
+        part = jnp.dot(h, d_buf[colour, :, at], preferred_element_type=jnp.float32)
+        o_buf[0, colour, :, :, at] = part.reshape(4, rows, tile).astype(jnp.bfloat16)
+        return 0
+
+    lax.fori_loop(0, 2 * steps, column, 0)
+    copy = pltpu.make_async_copy(o_buf, sent_ref, o_sem)
+    copy.start()
+    copy.wait()
+
+
+def hidden_call(place, spots, sources, gate_mat, up_mat, down_mat):
+    lines = sources[0].shape[0]
+    rows = lines // 4
     ff = gate_mat.shape[1]
     width = gate_mat.shape[0] // 4
     any_spec = pl.BlockSpec(memory_space=pl.ANY)
     return pl.pallas_call(
-        hidden_kernel,
-        out_shape=jax.ShapeDtypeStruct((2, 4, 4, rows, ff), jnp.bfloat16),
-        in_specs=[pl.BlockSpec(memory_space=pltpu.SMEM)] + [any_spec] * 22,
-        out_specs=pl.BlockSpec(memory_space=pltpu.VMEM),
+        functools.partial(hidden_kernel, len(sources), spots),
+        out_shape=[
+            jax.ShapeDtypeStruct((2, 4, 4, rows, ff), jnp.bfloat16),
+            jax.ShapeDtypeStruct((1, 2, 4, rows, width), jnp.bfloat16),
+        ],
+        in_specs=[pl.BlockSpec(memory_space=pltpu.SMEM)] + [any_spec] * (len(sources) + 3),
+        out_specs=[pl.BlockSpec(memory_space=pltpu.VMEM), any_spec],
         scratch_shapes=[
-            pltpu.VMEM((4, 4, 4, rows, width), jnp.bfloat16),
-            pltpu.VMEM((2, 2 * width, 2 * ff), jnp.bfloat16),
-            pltpu.VMEM((2, 4, 4, rows, 2 * ff), jnp.float32),
-            pltpu.VMEM((4, 4, rows, LANES), jnp.bfloat16),
+            pltpu.VMEM((4, 4, lines, width), jnp.bfloat16),
+            pltpu.VMEM((4, width, 2 * ff), jnp.bfloat16),
+            pltpu.VMEM((2, 4 * lines, 2 * ff), jnp.float32),
+            pltpu.VMEM((4, lines, LANES), jnp.bfloat16),
+            pltpu.VMEM((2, ff, width), jnp.bfloat16),
+            pltpu.VMEM((1, 2, 4, rows, width), jnp.bfloat16),
             pltpu.SemaphoreType.DMA((4, 4)),
+            pltpu.SemaphoreType.DMA((4,)),
+            pltpu.SemaphoreType.DMA,
             pltpu.SemaphoreType.DMA((2,)),
             pltpu.SemaphoreType.DMA,
         ],
-        compiler_params=pltpu.CompilerParams(vmem_limit_bytes=40 * 2**20),
+        compiler_params=pltpu.CompilerParams(vmem_limit_bytes=36 * 2**20),
         cost_estimate=pl.CostEstimate(
             flops=2 * 16 * rows * gate_mat.shape[0] * 2 * ff,
             bytes_accessed=24 * 2**20,
             transcendentals=0,
         ),
         name="hidden",
-    )(place, *own, *sibling, gate_mat, up_mat)
+    )(place, *sources, gate_mat, up_mat, down_mat)
 
 
 def down_kernel(offsets, adds, place_ref, h_ref, w_ref, *refs):
@@ -276,19 +315,23 @@
     )
 
     n_z = lax.axis_size("z")
+    cut = LANES + half // 2
     column = jnp.broadcast_to(block, (n_z, *block.shape))
     column = lax.all_to_all(column, "z", split_axis=0, concat_axis=0, tiled=True)
     column = column.reshape(-1, block.shape[1])
-    cut = LANES + half // 2
-    gathered = []
-    for part, (near, far) in ((column[:, :cut], ("x", "y")), (column[:, cut:], ("y", "x"))):
-        gathered.extend(far_gather(near_gather(part, near), far))
-    swapped = [shift(piece, "c", 1) for piece in gathered]
-    hidden = hidden_call(place, gathered, swapped, w_gate[0], w_up[0])
-
+    first = far_gather(near_gather(column[:, :cut], "x"), "y")
+    second = far_gather(near_gather(column[:, cut:], "y"), "x")
+    spots, sources = [], []
+    for side in range(2):
+        for colour, found in enumerate((first, second)):
+            for offset, row, piece in found:
+                at = offset * found[0][2].shape[0] + row
+                spots.append((side, colour, at, len(sources), 0, piece.shape[0]))
+                sources.append(shift(piece, "c", 1) if side else piece)
     down_mat = w_down[0]
+    hidden, far_sent = hidden_call(place, tuple(spots), sources, w_gate[0], w_up[0], down_mat)
+
     groups = ((2,), (0, 1, 3))
-    far_sent = down_call(place, hidden, down_mat, groups[0], None)[0]
     far_got = shift(far_sent, "c", 1)
     sent = down_call(place, hidden, down_mat, groups[1], None)[0]
     across = down_call(place, hidden, down_mat, groups[0], far_got)

time: 226 us -> 225 us (level)
  starting transfers between devices: 60.9 us -> 67.7 us
  Pallas kernels: 32 us -> 28.5 us
  waiting for transfers between devices: 73.3 us -> 70.2 us
    ppermute x42, starting transfers between devices: 60.9 us -> 67.7 us  [shift(): return lax.ppermute(value, axis, [(i, (i + step) % n) for i in range(n)])]
    ppermute x42, waiting for transfers between devices: 73.3 us -> 70.2 us  [shift(): return lax.ppermute(value, axis, [(i, (i + step) % n) for i in range(n)])]
    pallas_call x4 -> x3, Pallas kernels: 16.5 us -> 14.5 us  [down_call(): pl.pallas_call(functools.partial(down_kernel, offsets, adds), out_shape=[...]
    unnamed x36 -> x34, local copies, waits for them, and re-layouts: 16 us -> 14.9 us
  transfers between devices with their start and end apart: 42 -> 42, of which waited for: 21 -> 20; matrix products, arithmetic and copies ran while one was open for 2% -> 2% of each run, Pallas kernels for 5% -> 4%
where the time goes in v1:
time: 225 us; the launch traced here: 224 us
  waiting for transfers between devices  70.2 us (31%)
  starting transfers between devices  67.7 us (30%)
  blocking collectives  35.8 us (16%)
  Pallas kernels  28.5 us (13%)
  local copies, waits for them, and re-layouts  17.6 us (8%)
  other arithmetic  4.36 us (2%)
    ppermute x42, waiting for transfers between devices, shift(): return lax.ppermute(value, axis, [(i, (i + step) % n) for i in range(n)])  70.2 us
    ppermute x42, starting transfers between devices, shift(): return lax.ppermute(value, axis, [(i, (i + step) % n) for i in range(n)])  67.7 us
    all_to_all x2, blocking collectives, step(): lax.all_to_all(column, 'z', split_axis=0, concat_axis=0, tiled=True)  35.8 us
    unnamed x34, local copies, waits for them, and re-layouts  14.9 us
    pallas_call x3, Pallas kernels, down_call(): pl.pallas_call(functools.partial(down_kernel, offsets, adds), out_shape=[...  14.5 us
    pallas_call x1, Pallas kernels, hidden_call(): pl.pallas_call(functools.partial(hidden_kernel, len(sources), spots), out...  14.1 us
  transfers between devices with their start and end apart: 42, of which 20 were waited for; matrix products, arithmetic and copies ran while one was open for 2% of the time, Pallas kernels for 4%

profile of v1, /device:TPU:1, one launch (start us, length us, event | category | flops | bytes accessed | tf_op | source)
XLA Modules:
  0.0 224.4 jit_solution(12477781954612073463)
XLA Ops:
  1.7 3.2 %collective-permute-start = (bf16[4,3712]{1,0:T(4,128)(2,1)S(1)}, bf16[4,3712]{1,0:T(4,128)(2,1)S(1)}, u32[]{:S(2)}, u32[]{:S(2)}) collective-permute-start(bf16[4,3712]{1,0:T(4,128)(2,1)S(1)} %concatenate.44), channel_id=1, source_target_pairs={{0,1},{1,0},{2,3},{3,2},{4,5},{5,4},{6,7},{7,6},{8,9},{9,8},{10,11... | collective-permute-start | bytes 89096 | tf_op jit(solution)/shard_map/ppermute | solution.py:16
  5.9 21.9 %all_to_all.10 = bf16[8,8,3712]{2,1,0:T(8,128)(2,1)S(1)} all-to-all(bf16[8,8,3712]{2,1,0:T(8,128)(2,1)S(1)} %broadcast_in_dim.24), channel_id=1, replica_groups=mesh['z'=8,'y'=4,'x'=4,'c'=2] {'z'}, dimensions={0} | all-to-all | bytes 950272 | tf_op jit(solution)/shard_map/all_to_all | solution.py:320
  29.2 2.6 %collective-permute-start.9 = (bf16[64,1792]{1,0:T(8,128)(2,1)S(1)}, bf16[64,1792]{1,0:T(8,128)(2,1)S(1)}, u32[]{:S(2)}, u32[]{:S(2)}) collective-permute-start(bf16[64,1792]{1,0:T(8,128)(2,1)S(1)} %slice.143), channel_id=1, source_target_pairs={{0,16},{8,24},{16,0},{24,8},{1,17},{9,25},{17,1},{25,9},{2,18},{10... | collective-permute-start | bytes 688136 | tf_op jit(solution)/shard_map/ppermute | solution.py:16
  34.2 2.5 %collective-permute-start.2 = (bf16[64,1920]{1,0:T(8,128)(2,1)S(1)}, bf16[64,1920]{1,0:T(8,128)(2,1)S(1)}, u32[]{:S(2)}, u32[]{:S(2)}) collective-permute-start(bf16[64,1920]{1,0:T(8,128)(2,1)S(1)} %slice.140), channel_id=1, source_target_pairs={{0,4},{2,6},{4,0},{6,2},{1,5},{3,7},{5,1},{7,3},{8,12},{10,14},{12... | collective-permute-start | bytes 737288 | tf_op jit(solution)/shard_map/ppermute | solution.py:16
  37.8 2.9 %collective-permute-done.9 = bf16[64,1792]{1,0:T(8,128)(2,1)S(1)} collective-permute-done((bf16[64,1792]{1,0:T(8,128)(2,1)S(1)}, bf16[64,1792]{1,0:T(8,128)(2,1)S(1)}, u32[]{:S(2)}, u32[]{:S(2)}) %collective-permute-start.9) | collective-permute-done | bytes 229408 | tf_op jit(solution)/shard_map/ppermute | solution.py:16
  42.1 3.0 %collective-permute-done.2 = bf16[64,1920]{1,0:T(8,128)(2,1)S(1)} collective-permute-done((bf16[64,1920]{1,0:T(8,128)(2,1)S(1)}, bf16[64,1920]{1,0:T(8,128)(2,1)S(1)}, u32[]{:S(2)}, u32[]{:S(2)}) %collective-permute-start.2) | collective-permute-done | bytes 245792 | tf_op jit(solution)/shard_map/ppermute | solution.py:16
  45.7 2.3 %collective-permute-start.4 = (bf16[256,1920]{1,0:T(8,128)(2,1)S(1)}, bf16[256,1920]{1,0:T(8,128)(2,1)}, u32[]{:S(2)}, u32[]{:S(2)}) collective-permute-start(bf16[256,1920]{1,0:T(8,128)(2,1)S(1)} %pad_maximum_fusion.refs_0_), channel_id=1, source_target_pairs={{0,24},{8,0},{16,8},{24,16},{1,25},{9,1},{17,9},{25,17},{2,26},{10... | collective-permute-start | bytes 2949128 | tf_op jit(solution)/shard_map/ppermute | solution.py:16
  48.0 7.0 %collective-permute-start.15 = (bf16[256,1920]{1,0:T(8,128)(2,1)S(1)}, bf16[256,1920]{1,0:T(8,128)(2,1)S(1)}, u32[]{:S(2)}, u32[]{:S(2)}) collective-permute-start(bf16[256,1920]{1,0:T(8,128)(2,1)S(1)} %pad_maximum_fusion.refs_0_), channel_id=1, source_target_pairs={{0,1},{1,0},{2,3},{3,2},{4,5},{5,4},{6,7},{7,6},{8,9},{9,8},{10,11... | collective-permute-start | bytes 2949128 | tf_op jit(solution)/shard_map/ppermute | solution.py:16
  54.9 11.0 %collective-permute-done.12.refs_7_ = bf16[256,1792]{1,0:T(8,128)(2,1)S(1)} collective-permute-done((bf16[256,1792]{1,0:T(8,128)(2,1)S(1)}, bf16[256,1792]{1,0:T(8,128)(2,1)S(1)}, u32[]{:S(2)}, u32[]{:S(2)}) %collective-permute-start.12) | collective-permute-done | bytes 917536 | tf_op jit(solution)/shard_map/ppermute | solution.py:16
  65.9 2.0 collective-permute-start.20
  68.0 3.8 %collective-permute-start.13 = (bf16[128,1792]{1,0:T(8,128)(2,1)S(1)}, bf16[128,1792]{1,0:T(8,128)(2,1)S(1)}, u32[]{:S(2)}, u32[]{:S(2)}) collective-permute-start(bf16[128,1792]{1,0:T(8,128)(2,1)S(1)} %slice.144), channel_id=1, source_target_pairs={{0,2},{2,4},{4,6},{6,0},{1,3},{3,5},{5,7},{7,1},{8,10},{10,12},{12... | collective-permute-start | bytes 1376264 | tf_op jit(solution)/shard_map/ppermute | solution.py:16
  71.8 5.1 %collective-permute-done.11.refs_6_ = bf16[256,1792]{1,0:T(8,128)(2,1)} collective-permute-done((bf16[256,1792]{1,0:T(8,128)(2,1)S(1)}, bf16[256,1792]{1,0:T(8,128)(2,1)}, u32[]{:S(2)}, u32[]{:S(2)}) %collective-permute-start.11) | collective-permute-done | bytes 917536 | tf_op jit(solution)/shard_map/ppermute | solution.py:16
  79.1 2.8 %collective-permute-start.7 = (bf16[128,1920]{1,0:T(8,128)(2,1)S(1)}, bf16[128,1920]{1,0:T(8,128)(2,1)}, u32[]{:S(2)}, u32[]{:S(2)}) collective-permute-start(bf16[128,1920]{1,0:T(8,128)(2,1)S(1)} %slice.142), channel_id=1, source_target_pairs={{0,24},{8,0},{16,8},{24,16},{1,25},{9,1},{17,9},{25,17},{2,26},{10... | collective-permute-start | bytes 1474568 | tf_op jit(solution)/shard_map/ppermute | solution.py:16
  82.8 1.5 collective-permute-start.14
  87.5 6.0 %collective-permute-done.14.refs_9_ = bf16[128,1792]{1,0:T(8,128)(2,1)S(1)} collective-permute-done((bf16[128,1792]{1,0:T(8,128)(2,1)S(1)}, bf16[128,1792]{1,0:T(8,128)(2,1)S(1)}, u32[]{:S(2)}, u32[]{:S(2)}) %collective-permute-start.14) | collective-permute-done | bytes 458784 | tf_op jit(solution)/shard_map/ppermute | solution.py:16
  93.5 2.3 %collective-permute-start.17 = (bf16[256,1920]{1,0:T(8,128)(2,1)S(1)}, bf16[256,1920]{1,0:T(8,128)(2,1)}, u32[]{:S(2)}, u32[]{:S(2)}) collective-permute-start(bf16[256,1920]{1,0:T(8,128)(2,1)S(1)} %collective-permute-done.5.refs_2_), channel_id=1, source_target_pairs={{0,1},{1,0},{2,3},{3,2},{4,5},{5,4},{6,7},{7,6},{8,9},{9,8},{10,11... | collective-permute-start | bytes 2949128 | tf_op jit(solution)/shard_map/ppermute | solution.py:16
  111.8 14.1 %hidden.1 = (bf16[2,4,4,64,256]{4,3,2,1,0:T(8,128)(2,1)S(1)}, bf16[1,2,4,64,1792]{4,3,2,1,0:T(8,128)(2,1)S(1)}) custom-call(s32[2]{0:T(128)S(1)} %pad_add_fusion.place_ref, bf16[256,1920]{1,0:T(8,128)(2,1)S(1)} %pad_maximum_fusion.refs_0_, bf16[256,1920]{1,0:T(8,128)(2,1)} %collective-permute-done.4.refs_1_, ...), custom_call_target="tpu_custom_call" | custom-call | flops 7516192768 | bytes 25165824 | tf_op jit(solution)/shard_map/hidden/pallas_call | solution.py:159
  125.9 4.9 %down_send.1 = bf16[3,2,4,64,1792]{4,3,2,1,0:T(8,128)(2,1)S(1)} custom-call(s32[2]{0:T(128)S(1)} %pad_add_fusion.place_ref, bf16[2,4,4,64,256]{4,3,2,1,0:T(8,128)(2,1)S(1)} %get-tuple-element.17.h_ref, bf16[256,7168]{1,0:T(8,128)(2,1)S(1)} %bitcast.35), custom_call_target="tpu_custom_call" | custom-call | flops 1409286144 | bytes 5505024 | tf_op jit(solution)/shard_map/down_send/pallas_call | solution.py:268
  131.5 11.1 %collective-permute-done.26.refs_0_ = bf16[1,2,4,64,1792]{4,3,2,1,0:T(8,128)(2,1)S(1)} collective-permute-done((bf16[1,2,4,64,1792]{4,3,2,1,0:T(8,128)(2,1)S(1)}, bf16[1,2,4,64,1792]{4,3,2,1,0:T(8,128)(2,1)S(1)}, u32[]{:S(2)}, u32[]{:S(2)}) %collective-permute-start.26) | collective-permute-done | bytes 1835040 | tf_op jit(solution)/shard_map/ppermute | solution.py:16
  142.6 3.2 %down_add.3 = (bf16[2,64,1792]{2,1,0:T(8,128)(2,1)S(1)}, bf16[2,64,1792]{2,1,0:T(8,128)(2,1)S(1)}, bf16[2,64,1792]{2,1,0:T(8,128)(2,1)S(1)}, bf16[2,64,1792]{2,1,0:T(8,128)(2,1)S(1)}) custom-call(s32[2]{0:T(128)S(1)} %pad_add_fusion.place_ref, bf16[2,4,4,64,256]{4,3,2,1,0:T(8,128)(2,1)S(1)} %get-tuple-element.17.h_ref, bf16[256,7168]{1,0:T(8,128)(2,1)S(1)} %bitcast.36, ...), custom_call_target="tpu_custom_call" | custom-call | flops 469762048 | bytes 3670016 | tf_op jit(solution)/shard_map/down_add/pallas_call | solution.py:268
  145.8 2.8 %collective-permute-start.36 = (bf16[2,64,1792]{2,1,0:T(8,128)(2,1)S(1)}, bf16[2,64,1792]{2,1,0:T(8,128)(2,1)S(1)}, u32[]{:S(2)}, u32[]{:S(2)}) collective-permute-start(bf16[2,64,1792]{2,1,0:T(8,128)(2,1)S(1)} %get-tuple-element.28), channel_id=1, source_target_pairs={{0,6},{2,0},{4,2},{6,4},{1,7},{3,1},{5,3},{7,5},{8,14},{10,8},{12,... | collective-permute-start | bytes 1376264 | tf_op jit(solution)/shard_map/ppermute | solution.py:16
  148.6 2.7 %collective-permute-start.29 = (bf16[2,64,1792]{2,1,0:T(8,128)(2,1)S(1)}, bf16[2,64,1792]{2,1,0:T(8,128)(2,1)S(1)}, u32[]{:S(2)}, u32[]{:S(2)}) collective-permute-start(bf16[2,64,1792]{2,1,0:T(8,128)(2,1)S(1)} %get-tuple-element.23), channel_id=1, source_target_pairs={{0,24},{8,0},{16,8},{24,16},{1,25},{9,1},{17,9},{25,17},{2,26},{10... | collective-permute-start | bytes 1376264 | tf_op jit(solution)/shard_map/ppermute | solution.py:16
  151.3 6.3 %down_add.2 = (bf16[4,64,1792]{2,1,0:T(8,128)(2,1)S(1)}, bf16[4,64,1792]{2,1,0:T(8,128)(2,1)S(1)}, bf16[4,64,1792]{2,1,0:T(8,128)(2,1)S(1)}, bf16[4,64,1792]{2,1...) custom-call(s32[2]{0:T(128)S(1)} %pad_add_fusion.place_ref, ...), custom_call_target="tpu_custom_call" | custom-call | flops 1409286144 | bytes 11010048 | tf_op jit(solution)/shard_map/down_add/pallas_call | solution.py:268
  158.4 3.5 %collective-permute-start.37 = (bf16[4,64,1792]{2,1,0:T(8,128)(2,1)S(1)}, bf16[4,64,1792]{2,1,0:T(8,128)(2,1)S(1)}, u32[]{:S(2)}, u32[]{:S(2)}) collective-permute-start(bf16[4,64,1792]{2,1,0:T(8,128)(2,1)S(1)} %pad_maximum_fusion.5), channel_id=1, source_target_pairs={{0,6},{2,0},{4,2},{6,4},{1,7},{3,1},{5,3},{7,5},{8,14},{10,8},{12,... | collective-permute-start | bytes 2752520 | tf_op jit(solution)/shard_map/ppermute | solution.py:16
  165.8 14.6 %collective-permute-done.37 = bf16[4,64,1792]{2,1,0:T(8,128)(2,1)S(1)} collective-permute-done((bf16[4,64,1792]{2,1,0:T(8,128)(2,1)S(1)}, bf16[4,64,1792]{2,1,0:T(8,128)(2,1)S(1)}, u32[]{:S(2)}, u32[]{:S(2)}) %collective-permute-start.37) | collective-permute-done | bytes 917536 | tf_op jit(solution)/shard_map/ppermute | solution.py:16
  180.3 4.4 %collective-permute-done.35 = bf16[4,64,1792]{2,1,0:T(8,128)(2,1)S(1)} collective-permute-done((bf16[4,64,1792]{2,1,0:T(8,128)(2,1)S(1)}, bf16[4,64,1792]{2,1,0:T(8,128)(2,1)S(1)}, u32[]{:S(2)}, u32[]{:S(2)}) %collective-permute-start.35) | collective-permute-done | bytes 917536 | tf_op jit(solution)/shard_map/ppermute | solution.py:16
  185.2 2.7 %collective-permute-start.40 = (bf16[64,1792]{1,0:T(8,128)(2,1)S(1)}, bf16[64,1792]{1,0:T(8,128)(2,1)S(1)}, u32[]{:S(2)}, u32[]{:S(2)}) collective-permute-start(bf16[64,1792]{1,0:T(8,128)(2,1)S(1)} %get-tuple-element.33), channel_id=1, source_target_pairs={{0,24},{8,0},{16,8},{24,16},{1,25},{9,1},{17,9},{25,17},{2,26},{10... | collective-permute-start | bytes 688136 | tf_op jit(solution)/shard_map/ppermute | solution.py:16
  188.4 2.7 %collective-permute-start.33 = (bf16[64,1792]{1,0:T(8,128)(2,1)S(1)}, bf16[64,1792]{1,0:T(8,128)(2,1)S(1)}, u32[]{:S(2)}, u32[]{:S(2)}) collective-permute-start(bf16[64,1792]{1,0:T(8,128)(2,1)S(1)} %get-tuple-element.30), channel_id=1, source_target_pairs={{0,6},{2,0},{4,2},{6,4},{1,7},{3,1},{5,3},{7,5},{8,14},{10,8},{12,... | collective-permute-start | bytes 688136 | tf_op jit(solution)/shard_map/ppermute | solution.py:16
  192.0 1.7 collective-permute-done.40
  193.7 2.7 %collective-permute-done.39 = bf16[64,1792]{1,0:T(8,128)(2,1)S(1)} collective-permute-done((bf16[64,1792]{1,0:T(8,128)(2,1)S(1)}, bf16[64,1792]{1,0:T(8,128)(2,1)S(1)}, u32[]{:S(2)}, u32[]{:S(2)}) %collective-permute-start.39) | collective-permute-done | bytes 229408 | tf_op jit(solution)/shard_map/ppermute | solution.py:16
  198.1 13.8 %all_to_all.11 = bf16[8,8,3584]{2,1,0:T(8,128)(2,1)S(1)} all-to-all(bf16[8,8,3584]{2,1,0:T(8,128)(2,1)S(1)} %maximum_bitcast_fusion), channel_id=1, replica_groups=mesh['z'=8,'y'=4,'x'=4,'c'=2] {'z'}, dimensions={0} | all-to-all | bytes 917504 | tf_op jit(solution)/shard_map/all_to_all | solution.py:347
  212.1 10.9 %collective-permute-start.41 = (bf16[4,3584]{1,0:T(4,128)(2,1)S(1)}, bf16[4,3584]{1,0:T(4,128)(2,1)S(1)}, u32[]{:S(2)}, u32[]{:S(2)}) collective-permute-start(bf16[4,3584]{1,0:T(4,128)(2,1)S(1)} %get-tuple-element.36), channel_id=1, source_target_pairs={{0,1},{1,0},{2,3},{3,2},{4,5},{5,4},{6,7},{7,6},{8,9},{9,8},{10,11... | collective-permute-start | bytes 86024 | tf_op jit(solution)/shard_map/ppermute | solution.py:16
  (131 shorter events, 42.3 us)
Async XLA Ops:
  27.9 8.8 %collective-permute-start.10 = (bf16[64,1792]{1,0:T(8,128)(2,1)S(1)}, bf16[64,1792]{1,0:T(8,128)(2,1)S(1)}, u32[]{:S(2)}, u32[]{:S(2)}) collective-permute-start(bf16[64,1792]{1,0:T(8,128)(2,1)S(1)} %slice.143), channel_id=1, source_target_pairs={{0,8},{8,16},{16,24},{24,0},{1,9},{9,17},{17,25},{25,1},{2,10},{10... | collective-permute-start | bytes 688136 | tf_op jit(solution)/shard_map/ppermute | solution.py:16
  29.2 11.5 %collective-permute-start.9 = (bf16[64,1792]{1,0:T(8,128)(2,1)S(1)}, bf16[64,1792]{1,0:T(8,128)(2,1)S(1)}, u32[]{:S(2)}, u32[]{:S(2)}) collective-permute-start(bf16[64,1792]{1,0:T(8,128)(2,1)S(1)} %slice.143), channel_id=1, source_target_pairs={{0,16},{8,24},{16,0},{24,8},{1,17},{9,25},{17,1},{25,9},{2,18},{10... | collective-permute-start | bytes 688136 | tf_op jit(solution)/shard_map/ppermute | solution.py:16
  31.9 8.9 %collective-permute-start.8 = (bf16[64,1792]{1,0:T(8,128)(2,1)S(1)}, bf16[64,1792]{1,0:T(8,128)(2,1)S(1)}, u32[]{:S(2)}, u32[]{:S(2)}) collective-permute-start(bf16[64,1792]{1,0:T(8,128)(2,1)S(1)} %slice.143), channel_id=1, source_target_pairs={{0,24},{8,0},{16,8},{24,16},{1,25},{9,1},{17,9},{25,17},{2,26},{10... | collective-permute-start | bytes 688136 | tf_op jit(solution)/shard_map/ppermute | solution.py:16
  32.9 9.1 %collective-permute-start.3 = (bf16[64,1920]{1,0:T(8,128)(2,1)S(1)}, bf16[64,1920]{1,0:T(8,128)(2,1)S(1)}, u32[]{:S(2)}, u32[]{:S(2)}) collective-permute-start(bf16[64,1920]{1,0:T(8,128)(2,1)S(1)} %slice.140), channel_id=1, source_target_pairs={{0,2},{2,4},{4,6},{6,0},{1,3},{3,5},{5,7},{7,1},{8,10},{10,12},{12... | collective-permute-start | bytes 737288 | tf_op jit(solution)/shard_map/ppermute | solution.py:16
  34.2 10.9 %collective-permute-start.2 = (bf16[64,1920]{1,0:T(8,128)(2,1)S(1)}, bf16[64,1920]{1,0:T(8,128)(2,1)S(1)}, u32[]{:S(2)}, u32[]{:S(2)}) collective-permute-start(bf16[64,1920]{1,0:T(8,128)(2,1)S(1)} %slice.140), channel_id=1, source_target_pairs={{0,4},{2,6},{4,0},{6,2},{1,5},{3,7},{5,1},{7,3},{8,12},{10,14},{12... | collective-permute-start | bytes 737288 | tf_op jit(solution)/shard_map/ppermute | solution.py:16
  36.7 8.4 %collective-permute-start.1 = (bf16[64,1920]{1,0:T(8,128)(2,1)S(1)}, bf16[64,1920]{1,0:T(8,128)(2,1)S(1)}, u32[]{:S(2)}, u32[]{:S(2)}) collective-permute-start(bf16[64,1920]{1,0:T(8,128)(2,1)S(1)} %slice.140), channel_id=1, source_target_pairs={{0,6},{2,0},{4,2},{6,4},{1,7},{3,1},{5,3},{7,5},{8,14},{10,8},{12,... | collective-permute-start | bytes 737288 | tf_op jit(solution)/shard_map/ppermute | solution.py:16
  40.8 25.2 %collective-permute-start.12 = (bf16[256,1792]{1,0:T(8,128)(2,1)S(1)}, bf16[256,1792]{1,0:T(8,128)(2,1)S(1)}, u32[]{:S(2)}, u32[]{:S(2)}) collective-permute-start(bf16[256,1792]{1,0:T(8,128)(2,1)S(1)} %pad_maximum_fusion.1.refs_5_), channel_id=1, source_target_pairs={{0,2},{2,4},{4,6},{6,0},{1,3},{3,5},{5,7},{7,1},{8,10},{10,12},{12... | collective-permute-start | bytes 2752520 | tf_op jit(solution)/shard_map/ppermute | solution.py:16
  45.2 22.8 %collective-permute-start.5 = (bf16[256,1920]{1,0:T(8,128)(2,1)S(1)}, bf16[256,1920]{1,0:T(8,128)(2,1)S(1)}, u32[]{:S(2)}, u32[]{:S(2)}) collective-permute-start(bf16[256,1920]{1,0:T(8,128)(2,1)S(1)} %pad_maximum_fusion.refs_0_), channel_id=1, source_target_pairs={{0,8},{8,16},{16,24},{24,0},{1,9},{9,17},{17,25},{25,1},{2,10},{10... | collective-permute-start | bytes 2949128 | tf_op jit(solution)/shard_map/ppermute | solution.py:16
  45.7 32.3 %collective-permute-start.4 = (bf16[256,1920]{1,0:T(8,128)(2,1)S(1)}, bf16[256,1920]{1,0:T(8,128)(2,1)}, u32[]{:S(2)}, u32[]{:S(2)}) collective-permute-start(bf16[256,1920]{1,0:T(8,128)(2,1)S(1)} %pad_maximum_fusion.refs_0_), channel_id=1, source_target_pairs={{0,24},{8,0},{16,8},{24,16},{1,25},{9,1},{17,9},{25,17},{2,26},{10... | collective-permute-start | bytes 2949128 | tf_op jit(solution)/shard_map/ppermute | solution.py:16
  48.0 36.4 %collective-permute-start.15 = (bf16[256,1920]{1,0:T(8,128)(2,1)S(1)}, bf16[256,1920]{1,0:T(8,128)(2,1)S(1)}, u32[]{:S(2)}, u32[]{:S(2)}) collective-permute-start(bf16[256,1920]{1,0:T(8,128)(2,1)S(1)} %pad_maximum_fusion.refs_0_), channel_id=1, source_target_pairs={{0,1},{1,0},{2,3},{3,2},{4,5},{5,4},{6,7},{7,6},{8,9},{9,8},{10,11... | collective-permute-start | bytes 2949128 | tf_op jit(solution)/shard_map/ppermute | solution.py:16
  54.9 22.0 %collective-permute-start.11 = (bf16[256,1792]{1,0:T(8,128)(2,1)S(1)}, bf16[256,1792]{1,0:T(8,128)(2,1)}, u32[]{:S(2)}, u32[]{:S(2)}) collective-permute-start(bf16[256,1792]{1,0:T(8,128)(2,1)S(1)} %pad_maximum_fusion.1.refs_5_), channel_id=1, source_target_pairs={{0,6},{2,0},{4,2},{6,4},{1,7},{3,1},{5,3},{7,5},{8,14},{10,8},{12,... | collective-permute-start | bytes 2752520 | tf_op jit(solution)/shard_map/ppermute | solution.py:16
  65.9 15.9 %collective-permute-start.20 = (bf16[256,1792]{1,0:T(8,128)(2,1)S(1)}, bf16[256,1792]{1,0:T(8,128)(2,1)S(1)}, u32[]{:S(2)}, u32[]{:S(2)}) collective-permute-start(bf16[256,1792]{1,0:T(8,128)(2,1)S(1)} %pad_maximum_fusion.1.refs_5_), channel_id=1, source_target_pairs={{0,1},{1,0},{2,3},{3,2},{4,5},{5,4},{6,7},{7,6},{8,9},{9,8},{10,11... | collective-permute-start | bytes 2752520 | tf_op jit(solution)/shard_map/ppermute | solution.py:16
  68.0 18.7 %collective-permute-start.13 = (bf16[128,1792]{1,0:T(8,128)(2,1)S(1)}, bf16[128,1792]{1,0:T(8,128)(2,1)S(1)}, u32[]{:S(2)}, u32[]{:S(2)}) collective-permute-start(bf16[128,1792]{1,0:T(8,128)(2,1)S(1)} %slice.144), channel_id=1, source_target_pairs={{0,2},{2,4},{4,6},{6,0},{1,3},{3,5},{5,7},{7,1},{8,10},{10,12},{12... | collective-permute-start | bytes 1376264 | tf_op jit(solution)/shard_map/ppermute | solution.py:16
  76.9 18.8 %collective-permute-start.6 = (bf16[128,1920]{1,0:T(8,128)(2,1)S(1)}, bf16[128,1920]{1,0:T(8,128)(2,1)S(1)}, u32[]{:S(2)}, u32[]{:S(2)}) collective-permute-start(bf16[128,1920]{1,0:T(8,128)(2,1)S(1)} %slice.141), channel_id=1, source_target_pairs={{0,8},{8,16},{16,24},{24,0},{1,9},{9,17},{17,25},{25,1},{2,10},{10... | collective-permute-start | bytes 1474568 | tf_op jit(solution)/shard_map/ppermute | solution.py:16
  79.1 16.7 %collective-permute-start.7 = (bf16[128,1920]{1,0:T(8,128)(2,1)S(1)}, bf16[128,1920]{1,0:T(8,128)(2,1)}, u32[]{:S(2)}, u32[]{:S(2)}) collective-permute-start(bf16[128,1920]{1,0:T(8,128)(2,1)S(1)} %slice.142), channel_id=1, source_target_pairs={{0,24},{8,0},{16,8},{24,16},{1,25},{9,1},{17,9},{25,17},{2,26},{10... | collective-permute-start | bytes 1474568 | tf_op jit(solution)/shard_map/ppermute | solution.py:16
  82.8 10.7 %collective-permute-start.14 = (bf16[128,1792]{1,0:T(8,128)(2,1)S(1)}, bf16[128,1792]{1,0:T(8,128)(2,1)S(1)}, u32[]{:S(2)}, u32[]{:S(2)}) collective-permute-start(bf16[128,1792]{1,0:T(8,128)(2,1)S(1)} %slice.145), channel_id=1, source_target_pairs={{0,6},{2,0},{4,2},{6,4},{1,7},{3,1},{5,3},{7,5},{8,14},{10,8},{12,... | collective-permute-start | bytes 1376264 | tf_op jit(solution)/shard_map/ppermute | solution.py:16
  85.3 12.6 %collective-permute-start.22 = (bf16[256,1792]{1,0:T(8,128)(2,1)S(1)}, bf16[256,1792]{1,0:T(8,128)(2,1)S(1)}, u32[]{:S(2)}, u32[]{:S(2)}) collective-permute-start(bf16[256,1792]{1,0:T(8,128)(2,1)S(1)} %collective-permute-done.12.refs_7_), channel_id=1, source_target_pairs={{0,1},{1,0},{2,3},{3,2},{4,5},{5,4},{6,7},{7,6},{8,9},{9,8},{10,11... | collective-permute-start | bytes 2752520 | tf_op jit(solution)/shard_map/ppermute | solution.py:16
  86.7 10.4 %collective-permute-start.23 = (bf16[128,1792]{1,0:T(8,128)(2,1)S(1)}, bf16[128,1792]{1,0:T(8,128)(2,1)S(1)}, u32[]{:S(2)}, u32[]{:S(2)}) collective-permute-start(bf16[128,1792]{1,0:T(8,128)(2,1)S(1)} %collective-permute-done.13.refs_8_), channel_id=1, source_target_pairs={{0,1},{1,0},{2,3},{3,2},{4,5},{5,4},{6,7},{7,6},{8,9},{9,8},{10,11... | collective-permute-start | bytes 1376264 | tf_op jit(solution)/shard_map/ppermute | solution.py:16
  93.5 8.7 %collective-permute-start.17 = (bf16[256,1920]{1,0:T(8,128)(2,1)S(1)}, bf16[256,1920]{1,0:T(8,128)(2,1)}, u32[]{:S(2)}, u32[]{:S(2)}) collective-permute-start(bf16[256,1920]{1,0:T(8,128)(2,1)S(1)} %collective-permute-done.5.refs_2_), channel_id=1, source_target_pairs={{0,1},{1,0},{2,3},{3,2},{4,5},{5,4},{6,7},{7,6},{8,9},{9,8},{10,11... | collective-permute-start | bytes 2949128 | tf_op jit(solution)/shard_map/ppermute | solution.py:16
  130.9 20.4 %collective-permute-start.25 = (bf16[3,2,4,64,1792]{4,3,2,1,0:T(8,128)(2,1)S(1)}, bf16[3,2,4,64,1792]{4,3,2,1,0:T(8,128)(2,1)S(1)}, u32[]{:S(2)}, u32[]{:S(2)}) collective-permute-start(bf16[3,2,4,64,1792]{4,3,2,1,0:T(8,128)(2,1)S(1)} %down_send.1), channel_id=1, source_target_pairs={{0,1},{1,0},{2,3},{3,2},{4,5},{5,4},{6,7},{7,6},{8,9},{9,8},{10,11... | collective-permute-start | bytes 16515080 | tf_op jit(solution)/shard_map/ppermute | solution.py:16
  131.3 11.3 %collective-permute-start.26 = (bf16[1,2,4,64,1792]{4,3,2,1,0:T(8,128)(2,1)S(1)}, bf16[1,2,4,64,1792]{4,3,2,1,0:T(8,128)(2,1)S(1)}, u32[]{:S(2)}, u32[]{:S(2)}) collective-permute-start(bf16[1,2,4,64,1792]{4,3,2,1,0:T(8,128)(2,1)S(1)} %get-tuple-element.20), channel_id=1, source_target_pairs={{0,1},{1,0},{2,3},{3,2},{4,5},{5,4},{6,7},{7,6},{8,9},{9,8},{10,11... | collective-permute-start | bytes 5505032 | tf_op jit(solution)/shard_map/ppermute | solution.py:16
  145.8 12.3 %collective-permute-start.36 = (bf16[2,64,1792]{2,1,0:T(8,128)(2,1)S(1)}, bf16[2,64,1792]{2,1,0:T(8,128)(2,1)S(1)}, u32[]{:S(2)}, u32[]{:S(2)}) collective-permute-start(bf16[2,64,1792]{2,1,0:T(8,128)(2,1)S(1)} %get-tuple-element.28), channel_id=1, source_target_pairs={{0,6},{2,0},{4,2},{6,4},{1,7},{3,1},{5,3},{7,5},{8,14},{10,8},{12,... | collective-permute-start | bytes 1376264 | tf_op jit(solution)/shard_map/ppermute | solution.py:16
  148.6 15.7 %collective-permute-start.27 = (bf16[2,64,1792]{2,1,0:T(8,128)(2,1)S(1)}, bf16[2,64,1792]{2,1,0:T(8,128)(2,1)S(1)}, u32[]{:S(2)}, u32[]{:S(2)}) collective-permute-start(bf16[2,64,1792]{2,1,0:T(8,128)(2,1)S(1)} %get-tuple-element.21), channel_id=1, source_target_pairs={{0,8},{8,16},{16,24},{24,0},{1,9},{9,17},{17,25},{25,1},{2,10},{10... | collective-permute-start | bytes 1376264 | tf_op jit(solution)/shard_map/ppermute | solution.py:16
  148.6 15.1 %collective-permute-start.29 = (bf16[2,64,1792]{2,1,0:T(8,128)(2,1)S(1)}, bf16[2,64,1792]{2,1,0:T(8,128)(2,1)S(1)}, u32[]{:S(2)}, u32[]{:S(2)}) collective-permute-start(bf16[2,64,1792]{2,1,0:T(8,128)(2,1)S(1)} %get-tuple-element.23), channel_id=1, source_target_pairs={{0,24},{8,0},{16,8},{24,16},{1,25},{9,1},{17,9},{25,17},{2,26},{10... | collective-permute-start | bytes 1376264 | tf_op jit(solution)/shard_map/ppermute | solution.py:16
  151.3 12.1 %collective-permute-start.34 = (bf16[2,64,1792]{2,1,0:T(8,128)(2,1)S(1)}, bf16[2,64,1792]{2,1,0:T(8,128)(2,1)S(1)}, u32[]{:S(2)}, u32[]{:S(2)}) collective-permute-start(bf16[2,64,1792]{2,1,0:T(8,128)(2,1)S(1)} %get-tuple-element.26), channel_id=1, source_target_pairs={{0,2},{2,4},{4,6},{6,0},{1,3},{3,5},{5,7},{7,1},{8,10},{10,12},{12... | collective-permute-start | bytes 1376264 | tf_op jit(solution)/shard_map/ppermute | solution.py:16
  158.4 22.0 %collective-permute-start.37 = (bf16[4,64,1792]{2,1,0:T(8,128)(2,1)S(1)}, bf16[4,64,1792]{2,1,0:T(8,128)(2,1)S(1)}, u32[]{:S(2)}, u32[]{:S(2)}) collective-permute-start(bf16[4,64,1792]{2,1,0:T(8,128)(2,1)S(1)} %pad_maximum_fusion.5), channel_id=1, source_target_pairs={{0,6},{2,0},{4,2},{6,4},{1,7},{3,1},{5,3},{7,5},{8,14},{10,8},{12,... | collective-permute-start | bytes 2752520 | tf_op jit(solution)/shard_map/ppermute | solution.py:16
  163.6 21.1 %collective-permute-start.35 = (bf16[4,64,1792]{2,1,0:T(8,128)(2,1)S(1)}, bf16[4,64,1792]{2,1,0:T(8,128)(2,1)S(1)}, u32[]{:S(2)}, u32[]{:S(2)}) collective-permute-start(bf16[4,64,1792]{2,1,0:T(8,128)(2,1)S(1)} %pad_maximum_fusion.4), channel_id=1, source_target_pairs={{0,2},{2,4},{4,6},{6,0},{1,3},{3,5},{5,7},{7,1},{8,10},{10,12},{12... | collective-permute-start | bytes 2752520 | tf_op jit(solution)/shard_map/ppermute | solution.py:16
  163.9 23.9 %collective-permute-start.30 = (bf16[4,64,1792]{2,1,0:T(8,128)(2,1)S(1)}, bf16[4,64,1792]{2,1,0:T(8,128)(2,1)S(1)}, u32[]{:S(2)}, u32[]{:S(2)}) collective-permute-start(bf16[4,64,1792]{2,1,0:T(8,128)(2,1)S(1)} %pad_maximum_fusion.3), channel_id=1, source_target_pairs={{0,24},{8,0},{16,8},{24,16},{1,25},{9,1},{17,9},{25,17},{2,26},{10... | collective-permute-start | bytes 2752520 | tf_op jit(solution)/shard_map/ppermute | solution.py:16
  164.5 23.4 %collective-permute-start.28 = (bf16[4,64,1792]{2,1,0:T(8,128)(2,1)S(1)}, bf16[4,64,1792]{2,1,0:T(8,128)(2,1)S(1)}, u32[]{:S(2)}, u32[]{:S(2)}) collective-permute-start(bf16[4,64,1792]{2,1,0:T(8,128)(2,1)S(1)} %pad_maximum_fusion.2), channel_id=1, source_target_pairs={{0,8},{8,16},{16,24},{24,0},{1,9},{9,17},{17,25},{25,1},{2,10},{10... | collective-permute-start | bytes 2752520 | tf_op jit(solution)/shard_map/ppermute | solution.py:16
  185.2 8.5 %collective-permute-start.40 = (bf16[64,1792]{1,0:T(8,128)(2,1)S(1)}, bf16[64,1792]{1,0:T(8,128)(2,1)S(1)}, u32[]{:S(2)}, u32[]{:S(2)}) collective-permute-start(bf16[64,1792]{1,0:T(8,128)(2,1)S(1)} %get-tuple-element.33), channel_id=1, source_target_pairs={{0,24},{8,0},{16,8},{24,16},{1,25},{9,1},{17,9},{25,17},{2,26},{10... | collective-permute-start | bytes 688136 | tf_op jit(solution)/shard_map/ppermute | solution.py:16
  187.9 8.5 %collective-permute-start.39 = (bf16[64,1792]{1,0:T(8,128)(2,1)S(1)}, bf16[64,1792]{1,0:T(8,128)(2,1)S(1)}, u32[]{:S(2)}, u32[]{:S(2)}) collective-permute-start(bf16[64,1792]{1,0:T(8,128)(2,1)S(1)} %get-tuple-element.34), channel_id=1, source_target_pairs={{0,16},{8,24},{16,0},{24,8},{1,17},{9,25},{17,1},{25,9},{2,18},{10... | collective-permute-start | bytes 688136 | tf_op jit(solution)/shard_map/ppermute | solution.py:16
  212.1 11.7 %collective-permute-start.41 = (bf16[4,3584]{1,0:T(4,128)(2,1)S(1)}, bf16[4,3584]{1,0:T(4,128)(2,1)S(1)}, u32[]{:S(2)}, u32[]{:S(2)}) collective-permute-start(bf16[4,3584]{1,0:T(4,128)(2,1)S(1)} %get-tuple-element.36), channel_id=1, source_target_pairs={{0,1},{1,0},{2,3},{3,2},{4,5},{5,4},{6,7},{7,6},{8,9},{9,8},{10,11... | collective-permute-start | bytes 86024 | tf_op jit(solution)/shard_map/ppermute | solution.py:16
  (27 other events, 101.2 us)

commit v2 on v1

--- a/solution.py
+++ b/solution.py
@@ -56,9 +56,70 @@
     return jnp.where(core == 0, if_zero, if_one)
 
 
+def early_kernel(count, spots, place_ref, *refs):
+    sources, (gate_ref, up_ref, acc, x_buf, w_buf, x_sem, w_sem) = refs[:count], refs[count:]
+    lines, width = x_buf.shape[2:]
+    ff = gate_ref.shape[1]
+    core = place_ref[0]
+    for colour in range(2):
+        part = pl.ds(pl.multiple_of((2 * core + colour) * width, LANES), width)
+        for k, ref in enumerate((gate_ref, up_ref)):
+            pltpu.make_async_copy(
+                ref.at[part, :], w_buf.at[colour, :, k * ff : (k + 1) * ff], w_sem.at[colour]
+            ).start()
+        for i, (which, slot) in enumerate(spots):
+            if which == colour:
+                skip = sources[i].shape[1] - width
+                pltpu.make_async_copy(
+                    sources[i].at[:, skip : skip + width], x_buf.at[colour, slot], x_sem.at[colour, slot]
+                ).start()
+
+    def step(i, _):
+        colour, slot = i // 3, i % 3
+
+        @pl.when(slot == 0)
+        def _():
+            pltpu.make_async_copy(w_buf.at[colour], w_buf.at[colour], w_sem.at[colour]).wait()
+
+        there = x_buf.at[colour, slot]
+        pltpu.make_async_copy(there, there, x_sem.at[colour, slot]).wait()
+        at = pl.ds(pl.multiple_of((slot + slot // 2) * lines, 8), lines)
+        acc[colour, at, :] = jnp.dot(
+            x_buf[colour, slot], w_buf[colour], preferred_element_type=jnp.float32
+        )
+        return 0
+
+    lax.fori_loop(0, 6, step, 0)
+
+
+def early_call(place, spots, sources, gate_mat, up_mat):
+    lines = sources[0].shape[0]
+    ff = gate_mat.shape[1]
+    width = gate_mat.shape[0] // 4
+    any_spec = pl.BlockSpec(memory_space=pl.ANY)
+    return pl.pallas_call(
+        functools.partial(early_kernel, len(sources), spots),
+        out_shape=jax.ShapeDtypeStruct((2, 4 * lines, 2 * ff), jnp.float32),
+        in_specs=[pl.BlockSpec(memory_space=pltpu.SMEM)] + [any_spec] * (len(sources) + 2),
+        out_specs=pl.BlockSpec(memory_space=pltpu.VMEM),
+        scratch_shapes=[
+            pltpu.VMEM((2, 3, lines, width), jnp.bfloat16),
+            pltpu.VMEM((2, width, 2 * ff), jnp.bfloat16),
+            pltpu.SemaphoreType.DMA((2, 3)),
+            pltpu.SemaphoreType.DMA((2,)),
+        ],
+        compiler_params=pltpu.CompilerParams(vmem_limit_bytes=52 * 2**20),
+        cost_estimate=pl.CostEstimate(
+            flops=12 * lines * width * 2 * ff, bytes_accessed=9 * 2**20, transcendentals=0
+        ),
+        name="early",
+    )(place, *sources, gate_mat, up_mat)
+
+
 def hidden_kernel(count, spots, place_ref, *refs):
-    sources, (gate_ref, up_ref, down_ref, out_ref, sent_ref) = refs[:count], refs[count : count + 5]
-    x_buf, w_buf, acc, named, d_buf, o_buf, x_sem, w_sem, named_sem, d_sem, o_sem = refs[count + 5 :]
+    sources, refs = refs[:count], refs[count:]
+    gate_ref, up_ref, down_ref, early_ref, out_ref, sent_ref, x_buf, w_buf, acc, named = refs[:10]
+    d_buf, o_buf, x_sem, w_sem, named_sem, d_sem, o_sem, acc_sem = refs[10:]
     lines, width = x_buf.shape[2:]
     rows = lines // 4
     ff = gate_ref.shape[1]
@@ -74,7 +135,7 @@
                     w_sem.at[2 * side + colour],
                 ).start()
         for which, colour, first, source, begin, length in spots:
-            if which == side:
+            if which == side and (side == 1 or first // sources[0].shape[0] == 2):
                 skip = sources[source].shape[1] - width
                 block, row = first // lines, first % lines
                 pltpu.make_async_copy(
@@ -94,24 +155,35 @@
         part = pl.ds(pl.multiple_of((2 * (1 - core) + colour) * width, LANES), width)
         pltpu.make_async_copy(down_ref.at[:, part], d_buf.at[colour], d_sem.at[colour]).start()
 
+    kept = ((0, 2), (3, 1))
+    for begin, size in kept:
+        at = slice(begin * lines, (begin + size) * lines)
+        pltpu.make_async_copy(early_ref.at[:, at], acc.at[:, at], acc_sem.at[size - 1]).start()
+
     def step(i, _):
-        group, pair = i // 2, i % 2
-        side, colour = group // 2, group % 2
-
-        @pl.when(pair == 0)
+        early = i < 2
+        group = jnp.where(early, i, 2 + (i - 2) // 4)
+        block = jnp.where(early, 2, (i - 2) % 4)
+        colour = group % 2
+
+        @pl.when(early | (i == 2) | (i == 6))
         def _():
             pltpu.make_async_copy(w_buf.at[group], w_buf.at[group], w_sem.at[group]).wait()
 
-        for block in range(2):
-            there = x_buf.at[group, 2 * pair + block]
-            pltpu.make_async_copy(there, there, x_sem.at[group, 2 * pair + block]).wait()
-        x = x_buf[group, pl.ds(2 * pair, 2)].reshape(2 * lines, width)
-        part = jnp.dot(x, w_buf[group], preferred_element_type=jnp.float32)
-        at = pl.ds(pl.multiple_of(2 * pair * lines, 8), 2 * lines)
-        acc[colour, at, :] = jnp.where(side == 0, part, part + acc[colour, at, :])
+        @pl.when(i == 2)
+        def _():
+            for begin, size in kept:
+                there = acc.at[:, begin * lines : (begin + size) * lines]
+                pltpu.make_async_copy(there, there, acc_sem.at[size - 1]).wait()
+
+        there = x_buf.at[group, block]
+        pltpu.make_async_copy(there, there, x_sem.at[group, block]).wait()
+        part = jnp.dot(x_buf[group, block], w_buf[group], preferred_element_type=jnp.float32)
+        at = pl.ds(pl.multiple_of(block * lines, 8), lines)
+        acc[colour, at, :] = jnp.where(early, part, part + acc[colour, at, :])
         return 0
 
-    lax.fori_loop(0, 8, step, 0)
+    lax.fori_loop(0, 10, step, 0)
     pltpu.make_async_copy(named, named, named_sem).wait()
     lane = lax.broadcasted_iota(jnp.int32, (LANES, ff), 0)
     chosen = ((lane == expert) | (lane == expert + LANES // 2)).astype(jnp.bfloat16)
@@ -150,7 +222,7 @@
     copy.wait()
 
 
-def hidden_call(place, spots, sources, gate_mat, up_mat, down_mat):
+def hidden_call(place, spots, sources, gate_mat, up_mat, down_mat, early):
     lines = sources[0].shape[0]
     rows = lines // 4
     ff = gate_mat.shape[1]
@@ -162,7 +234,7 @@
             jax.ShapeDtypeStruct((2, 4, 4, rows, ff), jnp.bfloat16),
             jax.ShapeDtypeStruct((1, 2, 4, rows, width), jnp.bfloat16),
         ],
-        in_specs=[pl.BlockSpec(memory_space=pltpu.SMEM)] + [any_spec] * (len(sources) + 3),
+        in_specs=[pl.BlockSpec(memory_space=pltpu.SMEM)] + [any_spec] * (len(sources) + 4),
         out_specs=[pl.BlockSpec(memory_space=pltpu.VMEM), any_spec],
         scratch_shapes=[
             pltpu.VMEM((4, 4, lines, width), jnp.bfloat16),
@@ -176,6 +248,7 @@
             pltpu.SemaphoreType.DMA,
             pltpu.SemaphoreType.DMA((2,)),
             pltpu.SemaphoreType.DMA,
+            pltpu.SemaphoreType.DMA((2,)),
         ],
         compiler_params=pltpu.CompilerParams(vmem_limit_bytes=36 * 2**20),
         cost_estimate=pl.CostEstimate(
@@ -184,7 +257,7 @@
             transcendentals=0,
         ),
         name="hidden",
-    )(place, *sources, gate_mat, up_mat, down_mat)
+    )(place, *sources, gate_mat, up_mat, down_mat, early)
 
 
 def down_kernel(offsets, adds, place_ref, h_ref, w_ref, *refs):
@@ -329,7 +402,13 @@
                 spots.append((side, colour, at, len(sources), 0, piece.shape[0]))
                 sources.append(shift(piece, "c", 1) if side else piece)
     down_mat = w_down[0]
-    hidden, far_sent = hidden_call(place, tuple(spots), sources, w_gate[0], w_up[0], down_mat)
+    parts = [(c, (0, 1, 3).index(k), p) for c, f in enumerate((first, second)) for k, _, p in f if k != 2]
+    early = early_call(
+        place, tuple(p[:2] for p in parts), [p[2] for p in parts], w_gate[0], w_up[0]
+    )
+    hidden, far_sent = hidden_call(
+        place, tuple(spots), sources, w_gate[0], w_up[0], down_mat, early
+    )
 
     groups = ((2,), (0, 1, 3))
     far_got = shift(far_sent, "c", 1)

time: 225 us -> 229 us (1.018)
  Pallas kernels: 28.5 us -> 36.6 us
  local copies, waits for them, and re-layouts: 17.6 us -> 15.2 us
    pallas_call x0 -> x1, Pallas kernels: none -> 8.48 us  [early_call(): pl.pallas_call(functools.partial(early_kernel, len(sources), spots), out_...]
    unnamed x34 -> x42, local copies, waits for them, and re-layouts: 14.9 us -> 12.5 us
  transfers between devices with their start and end apart: 42 -> 42, of which waited for: 20 -> 17; matrix products, arithmetic and copies ran while one was open for 2% -> 2% of each run, Pallas kernels for 4% -> 8%
where the time goes in v2:
time: 229 us
  waiting for transfers between devices  70.2 us (31%)
  starting transfers between devices  66.3 us (29%)
  Pallas kernels  36.6 us (16%)
  blocking collectives  35.8 us (16%)
  local copies, waits for them, and re-layouts  15.2 us (7%)
  other arithmetic  4.34 us (2%)
    ppermute x42, waiting for transfers between devices, shift(): return lax.ppermute(value, axis, [(i, (i + step) % n) for i in range(n)])  70.2 us
    ppermute x42, starting transfers between devices, shift(): return lax.ppermute(value, axis, [(i, (i + step) % n) for i in range(n)])  66.3 us
    all_to_all x2, blocking collectives, step(): lax.all_to_all(column, 'z', split_axis=0, concat_axis=0, tiled=True)  35.8 us
    pallas_call x3, Pallas kernels, down_call(): pl.pallas_call(functools.partial(down_kernel, offsets, adds), out_shape=[...  14.5 us
    pallas_call x1, Pallas kernels, hidden_call(): pl.pallas_call(functools.partial(hidden_kernel, len(sources), spots), out...  13.7 us
    unnamed x42, local copies, waits for them, and re-layouts  12.5 us
    pallas_call x1, Pallas kernels, early_call(): pl.pallas_call(functools.partial(early_kernel, len(sources), spots), out_...  8.48 us
  transfers between devices with their start and end apart: 42, of which 17 were waited for; matrix products, arithmetic and copies ran while one was open for 2% of the time, Pallas kernels for 8%

profile of v2, /device:TPU:1, one launch (start us, length us, event | category | flops | bytes accessed | tf_op | source)
XLA Modules:
  0.0 228.9 jit_solution(4279091607022770645)
XLA Ops:
  1.7 3.2 %collective-permute-start = (bf16[4,3712]{1,0:T(4,128)(2,1)S(1)}, bf16[4,3712]{1,0:T(4,128)(2,1)S(1)}, u32[]{:S(2)}, u32[]{:S(2)}) collective-permute-start(bf16[4,3712]{1,0:T(4,128)(2,1)S(1)} %concatenate.44), channel_id=1, source_target_pairs={{0,1},{1,0},{2,3},{3,2},{4,5},{5,4},{6,7},{7,6},{8,9},{9,8},{10,11... | collective-permute-start | bytes 89096 | tf_op jit(solution)/shard_map/ppermute | solution.py:16
  5.9 21.9 %all_to_all.10 = bf16[8,8,3712]{2,1,0:T(8,128)(2,1)S(1)} all-to-all(bf16[8,8,3712]{2,1,0:T(8,128)(2,1)S(1)} %broadcast_in_dim.24), channel_id=1, replica_groups=mesh['z'=8,'y'=4,'x'=4,'c'=2] {'z'}, dimensions={0} | all-to-all | bytes 950272 | tf_op jit(solution)/shard_map/all_to_all | solution.py:393
  29.2 2.6 %collective-permute-start.9 = (bf16[64,1792]{1,0:T(8,128)(2,1)S(1)}, bf16[64,1792]{1,0:T(8,128)(2,1)S(1)}, u32[]{:S(2)}, u32[]{:S(2)}) collective-permute-start(bf16[64,1792]{1,0:T(8,128)(2,1)S(1)} %slice.143), channel_id=1, source_target_pairs={{0,16},{8,24},{16,0},{24,8},{1,17},{9,25},{17,1},{25,9},{2,18},{10... | collective-permute-start | bytes 688136 | tf_op jit(solution)/shard_map/ppermute | solution.py:16
  34.2 2.5 %collective-permute-start.2 = (bf16[64,1920]{1,0:T(8,128)(2,1)S(1)}, bf16[64,1920]{1,0:T(8,128)(2,1)S(1)}, u32[]{:S(2)}, u32[]{:S(2)}) collective-permute-start(bf16[64,1920]{1,0:T(8,128)(2,1)S(1)} %slice.140), channel_id=1, source_target_pairs={{0,4},{2,6},{4,0},{6,2},{1,5},{3,7},{5,1},{7,3},{8,12},{10,14},{12... | collective-permute-start | bytes 737288 | tf_op jit(solution)/shard_map/ppermute | solution.py:16
  37.8 2.9 %collective-permute-done.9 = bf16[64,1792]{1,0:T(8,128)(2,1)S(1)} collective-permute-done((bf16[64,1792]{1,0:T(8,128)(2,1)S(1)}, bf16[64,1792]{1,0:T(8,128)(2,1)S(1)}, u32[]{:S(2)}, u32[]{:S(2)}) %collective-permute-start.9) | collective-permute-done | bytes 229408 | tf_op jit(solution)/shard_map/ppermute | solution.py:16
  42.1 3.0 %collective-permute-done.2 = bf16[64,1920]{1,0:T(8,128)(2,1)S(1)} collective-permute-done((bf16[64,1920]{1,0:T(8,128)(2,1)S(1)}, bf16[64,1920]{1,0:T(8,128)(2,1)S(1)}, u32[]{:S(2)}, u32[]{:S(2)}) %collective-permute-start.2) | collective-permute-done | bytes 245792 | tf_op jit(solution)/shard_map/ppermute | solution.py:16
  45.7 2.3 %collective-permute-start.4 = (bf16[256,1920]{1,0:T(8,128)(2,1)S(1)}, bf16[256,1920]{1,0:T(8,128)(2,1)}, u32[]{:S(2)}, u32[]{:S(2)}) collective-permute-start(bf16[256,1920]{1,0:T(8,128)(2,1)S(1)} %pad_maximum_fusion.refs_0_), channel_id=1, source_target_pairs={{0,24},{8,0},{16,8},{24,16},{1,25},{9,1},{17,9},{25,17},{2,26},{10... | collective-permute-start | bytes 2949128 | tf_op jit(solution)/shard_map/ppermute | solution.py:16
  48.0 7.0 %collective-permute-start.15 = (bf16[256,1920]{1,0:T(8,128)(2,1)S(1)}, bf16[256,1920]{1,0:T(8,128)(2,1)S(1)}, u32[]{:S(2)}, u32[]{:S(2)}) collective-permute-start(bf16[256,1920]{1,0:T(8,128)(2,1)S(1)} %pad_maximum_fusion.refs_0_), channel_id=1, source_target_pairs={{0,1},{1,0},{2,3},{3,2},{4,5},{5,4},{6,7},{7,6},{8,9},{9,8},{10,11... | collective-permute-start | bytes 2949128 | tf_op jit(solution)/shard_map/ppermute | solution.py:16
  55.0 11.0 %collective-permute-done.12.refs_5_.refs_7_ = bf16[256,1792]{1,0:T(8,128)(2,1)S(1)} collective-permute-done((bf16[256,1792]{1,0:T(8,128)(2,1)S(1)}, bf16[256,1792]{1,0:T(8,128)(2,1)S(1)}, u32[]{:S(2)}, u32[]{:S(2)}) %collective-permute-start.12) | collective-permute-done | bytes 917536 | tf_op jit(solution)/shard_map/ppermute | solution.py:16
  68.0 3.8 %collective-permute-start.13 = (bf16[128,1792]{1,0:T(8,128)(2,1)S(1)}, bf16[128,1792]{1,0:T(8,128)(2,1)S(1)}, u32[]{:S(2)}, u32[]{:S(2)}) collective-permute-start(bf16[128,1792]{1,0:T(8,128)(2,1)S(1)} %slice.144), channel_id=1, source_target_pairs={{0,2},{2,4},{4,6},{6,0},{1,3},{3,5},{5,7},{7,1},{8,10},{10,12},{12... | collective-permute-start | bytes 1376264 | tf_op jit(solution)/shard_map/ppermute | solution.py:16
  71.8 5.1 %collective-permute-done.11.refs_4_.refs_6_ = bf16[256,1792]{1,0:T(8,128)(2,1)} collective-permute-done((bf16[256,1792]{1,0:T(8,128)(2,1)S(1)}, bf16[256,1792]{1,0:T(8,128)(2,1)}, u32[]{:S(2)}, u32[]{:S(2)}) %collective-permute-start.11) | collective-permute-done | bytes 917536 | tf_op jit(solution)/shard_map/ppermute | solution.py:16
  79.1 2.8 %collective-permute-start.7 = (bf16[128,1920]{1,0:T(8,128)(2,1)S(1)}, bf16[128,1920]{1,0:T(8,128)(2,1)}, u32[]{:S(2)}, u32[]{:S(2)}) collective-permute-start(bf16[128,1920]{1,0:T(8,128)(2,1)S(1)} %slice.142), channel_id=1, source_target_pairs={{0,24},{8,0},{16,8},{24,16},{1,25},{9,1},{17,9},{25,17},{2,26},{10... | collective-permute-start | bytes 1474568 | tf_op jit(solution)/shard_map/ppermute | solution.py:16
  87.5 6.0 %collective-permute-done.14.refs_9_ = bf16[128,1792]{1,0:T(8,128)(2,1)S(1)} collective-permute-done((bf16[128,1792]{1,0:T(8,128)(2,1)S(1)}, bf16[128,1792]{1,0:T(8,128)(2,1)S(1)}, u32[]{:S(2)}, u32[]{:S(2)}) %collective-permute-start.14) | collective-permute-done | bytes 458784 | tf_op jit(solution)/shard_map/ppermute | solution.py:16
  93.5 2.3 collective-permute-start.17
  101.3 8.5 %early.1.refs_23_ = f32[2,1024,512]{2,1,0:T(8,128)} custom-call(s32[2]{0:T(128)S(1)} %pad_add_fusion.place_ref, bf16[256,1920]{1,0:T(8,128)(2,1)} %copy-done.1, bf16[256,1920]{1,0:T(8,128)(2,1)} %collective-permute-done.4.refs_1_, bf16[256,1920]{1,0:T(8,128)(2,1)} %copy-done.3, bf16[256,1792]{1,0:T(8,128)(2,1)S(1)} %pad_maximum_fusion.1.refs_3_.refs_5_, ...), custom_call_target="tpu_custom_call" | custom-call | flops 2818572288 | bytes 9437184 | tf_op jit(solution)/shard_map/early/pallas_call | solution.py:100
  116.3 13.7 %hidden.1 = (bf16[2,4,4,64,256]{4,3,2,1,0:T(8,128)(2,1)S(1)}, bf16[1,2,4,64,1792]{4,3,2,1,0:T(8,128)(2,1)S(1)}) custom-call(s32[2]{0:T(128)S(1)} %pad_add_fusion.place_ref, bf16[256,1920]{1,0:T(8,128)(2,1)S(1)} %copy-done.2, bf16[256,1920]{1,0:T(8,128)(2,1)} %collective-permute-done.4.refs_1_, bf16[256,1920]{1,0:T(8,128)(2,1)S(1)} %copy-done.4, ...), custom_call_target="tpu_custom_call" | custom-call | flops 7516192768 | bytes 25165824 | tf_op jit(solution)/shard_map/hidden/pallas_call | solution.py:231
  130.0 4.9 %down_send.1 = bf16[3,2,4,64,1792]{4,3,2,1,0:T(8,128)(2,1)S(1)} custom-call(s32[2]{0:T(128)S(1)} %pad_add_fusion.place_ref, bf16[2,4,4,64,256]{4,3,2,1,0:T(8,128)(2,1)S(1)} %get-tuple-element.17.h_ref, bf16[256,7168]{1,0:T(8,128)(2,1)S(1)} %bitcast.35), custom_call_target="tpu_custom_call" | custom-call | flops 1409286144 | bytes 5505024 | tf_op jit(solution)/shard_map/down_send/pallas_call | solution.py:341
  135.6 11.1 %collective-permute-done.26.refs_0_ = bf16[1,2,4,64,1792]{4,3,2,1,0:T(8,128)(2,1)S(1)} collective-permute-done((bf16[1,2,4,64,1792]{4,3,2,1,0:T(8,128)(2,1)S(1)}, bf16[1,2,4,64,1792]{4,3,2,1,0:T(8,128)(2,1)S(1)}, u32[]{:S(2)}, u32[]{:S(2)}) %collective-permute-start.26) | collective-permute-done | bytes 1835040 | tf_op jit(solution)/shard_map/ppermute | solution.py:16
  146.7 3.2 %down_add.3 = (bf16[2,64,1792]{2,1,0:T(8,128)(2,1)S(1)}, bf16[2,64,1792]{2,1,0:T(8,128)(2,1)S(1)}, bf16[2,64,1792]{2,1,0:T(8,128)(2,1)S(1)}, bf16[2,64,1792]{2,1,0:T(8,128)(2,1)S(1)}) custom-call(s32[2]{0:T(128)S(1)} %pad_add_fusion.place_ref, bf16[2,4,4,64,256]{4,3,2,1,0:T(8,128)(2,1)S(1)} %get-tuple-element.17.h_ref, bf16[256,7168]{1,0:T(8,128)(2,1)S(1)} %bitcast.36, ...), custom_call_target="tpu_custom_call" | custom-call | flops 469762048 | bytes 3670016 | tf_op jit(solution)/shard_map/down_add/pallas_call | solution.py:341
  149.9 2.8 %collective-permute-start.36 = (bf16[2,64,1792]{2,1,0:T(8,128)(2,1)S(1)}, bf16[2,64,1792]{2,1,0:T(8,128)(2,1)S(1)}, u32[]{:S(2)}, u32[]{:S(2)}) collective-permute-start(bf16[2,64,1792]{2,1,0:T(8,128)(2,1)S(1)} %get-tuple-element.28), channel_id=1, source_target_pairs={{0,6},{2,0},{4,2},{6,4},{1,7},{3,1},{5,3},{7,5},{8,14},{10,8},{12,... | collective-permute-start | bytes 1376264 | tf_op jit(solution)/shard_map/ppermute | solution.py:16
  152.7 2.7 %collective-permute-start.29 = (bf16[2,64,1792]{2,1,0:T(8,128)(2,1)S(1)}, bf16[2,64,1792]{2,1,0:T(8,128)(2,1)S(1)}, u32[]{:S(2)}, u32[]{:S(2)}) collective-permute-start(bf16[2,64,1792]{2,1,0:T(8,128)(2,1)S(1)} %get-tuple-element.23), channel_id=1, source_target_pairs={{0,24},{8,0},{16,8},{24,16},{1,25},{9,1},{17,9},{25,17},{2,26},{10... | collective-permute-start | bytes 1376264 | tf_op jit(solution)/shard_map/ppermute | solution.py:16
  155.4 6.3 %down_add.2 = (bf16[4,64,1792]{2,1,0:T(8,128)(2,1)S(1)}, bf16[4,64,1792]{2,1,0:T(8,128)(2,1)S(1)}, bf16[4,64,1792]{2,1,0:T(8,128)(2,1)S(1)}, bf16[4,64,1792]{2,1...) custom-call(s32[2]{0:T(128)S(1)} %pad_add_fusion.place_ref, ...), custom_call_target="tpu_custom_call" | custom-call | flops 1409286144 | bytes 11010048 | tf_op jit(solution)/shard_map/down_add/pallas_call | solution.py:341
  162.7 3.5 %collective-permute-start.37 = (bf16[4,64,1792]{2,1,0:T(8,128)(2,1)S(1)}, bf16[4,64,1792]{2,1,0:T(8,128)(2,1)S(1)}, u32[]{:S(2)}, u32[]{:S(2)}) collective-permute-start(bf16[4,64,1792]{2,1,0:T(8,128)(2,1)S(1)} %pad_maximum_fusion.5), channel_id=1, source_target_pairs={{0,6},{2,0},{4,2},{6,4},{1,7},{3,1},{5,3},{7,5},{8,14},{10,8},{12,... | collective-permute-start | bytes 2752520 | tf_op jit(solution)/shard_map/ppermute | solution.py:16
  170.1 14.8 %collective-permute-done.37 = bf16[4,64,1792]{2,1,0:T(8,128)(2,1)S(1)} collective-permute-done((bf16[4,64,1792]{2,1,0:T(8,128)(2,1)S(1)}, bf16[4,64,1792]{2,1,0:T(8,128)(2,1)S(1)}, u32[]{:S(2)}, u32[]{:S(2)}) %collective-permute-start.37) | collective-permute-done | bytes 917536 | tf_op jit(solution)/shard_map/ppermute | solution.py:16
  184.9 4.4 %collective-permute-done.35 = bf16[4,64,1792]{2,1,0:T(8,128)(2,1)S(1)} collective-permute-done((bf16[4,64,1792]{2,1,0:T(8,128)(2,1)S(1)}, bf16[4,64,1792]{2,1,0:T(8,128)(2,1)S(1)}, u32[]{:S(2)}, u32[]{:S(2)}) %collective-permute-start.35) | collective-permute-done | bytes 917536 | tf_op jit(solution)/shard_map/ppermute | solution.py:16
  189.8 2.7 %collective-permute-start.40 = (bf16[64,1792]{1,0:T(8,128)(2,1)S(1)}, bf16[64,1792]{1,0:T(8,128)(2,1)S(1)}, u32[]{:S(2)}, u32[]{:S(2)}) collective-permute-start(bf16[64,1792]{1,0:T(8,128)(2,1)S(1)} %get-tuple-element.33), channel_id=1, source_target_pairs={{0,24},{8,0},{16,8},{24,16},{1,25},{9,1},{17,9},{25,17},{2,26},{10... | collective-permute-start | bytes 688136 | tf_op jit(solution)/shard_map/ppermute | solution.py:16
  193.0 2.7 %collective-permute-start.33 = (bf16[64,1792]{1,0:T(8,128)(2,1)S(1)}, bf16[64,1792]{1,0:T(8,128)(2,1)S(1)}, u32[]{:S(2)}, u32[]{:S(2)}) collective-permute-start(bf16[64,1792]{1,0:T(8,128)(2,1)S(1)} %get-tuple-element.30), channel_id=1, source_target_pairs={{0,6},{2,0},{4,2},{6,4},{1,7},{3,1},{5,3},{7,5},{8,14},{10,8},{12,... | collective-permute-start | bytes 688136 | tf_op jit(solution)/shard_map/ppermute | solution.py:16
  196.0 2.1 collective-permute-done.40
  198.1 2.6 %collective-permute-done.39 = bf16[64,1792]{1,0:T(8,128)(2,1)S(1)} collective-permute-done((bf16[64,1792]{1,0:T(8,128)(2,1)S(1)}, bf16[64,1792]{1,0:T(8,128)(2,1)S(1)}, u32[]{:S(2)}, u32[]{:S(2)}) %collective-permute-start.39) | collective-permute-done | bytes 229408 | tf_op jit(solution)/shard_map/ppermute | solution.py:16
  200.9 2.3 %collective-permute-done.32 = bf16[64,1792]{1,0:T(8,128)(2,1)S(1)} collective-permute-done((bf16[64,1792]{1,0:T(8,128)(2,1)S(1)}, bf16[64,1792]{1,0:T(8,128)(2,1)S(1)}, u32[]{:S(2)}, u32[]{:S(2)}) %collective-permute-start.32) | collective-permute-done | bytes 229408 | tf_op jit(solution)/shard_map/ppermute | solution.py:16
  203.4 13.8 %all_to_all.11 = bf16[8,8,3584]{2,1,0:T(8,128)(2,1)S(1)} all-to-all(bf16[8,8,3584]{2,1,0:T(8,128)(2,1)S(1)} %maximum_bitcast_fusion), channel_id=1, replica_groups=mesh['z'=8,'y'=4,'x'=4,'c'=2] {'z'}, dimensions={0} | all-to-all | bytes 917504 | tf_op jit(solution)/shard_map/all_to_all | solution.py:426
  217.4 10.0 %collective-permute-start.41 = (bf16[4,3584]{1,0:T(4,128)(2,1)S(1)}, bf16[4,3584]{1,0:T(4,128)(2,1)S(1)}, u32[]{:S(2)}, u32[]{:S(2)}) collective-permute-start(bf16[4,3584]{1,0:T(4,128)(2,1)S(1)} %get-tuple-element.36), channel_id=1, source_target_pairs={{0,1},{1,0},{2,3},{3,2},{4,5},{5,4},{6,7},{7,6},{8,9},{9,8},{10,11... | collective-permute-start | bytes 86024 | tf_op jit(solution)/shard_map/ppermute | solution.py:16
  (140 shorter events, 39.9 us)
Async XLA Ops:
  29.2 11.5 %collective-permute-start.9 = (bf16[64,1792]{1,0:T(8,128)(2,1)S(1)}, bf16[64,1792]{1,0:T(8,128)(2,1)S(1)}, u32[]{:S(2)}, u32[]{:S(2)}) collective-permute-start(bf16[64,1792]{1,0:T(8,128)(2,1)S(1)} %slice.143), channel_id=1, source_target_pairs={{0,16},{8,24},{16,0},{24,8},{1,17},{9,25},{17,1},{25,9},{2,18},{10... | collective-permute-start | bytes 688136 | tf_op jit(solution)/shard_map/ppermute | solution.py:16
  31.9 8.9 %collective-permute-start.8 = (bf16[64,1792]{1,0:T(8,128)(2,1)S(1)}, bf16[64,1792]{1,0:T(8,128)(2,1)S(1)}, u32[]{:S(2)}, u32[]{:S(2)}) collective-permute-start(bf16[64,1792]{1,0:T(8,128)(2,1)S(1)} %slice.143), channel_id=1, source_target_pairs={{0,24},{8,0},{16,8},{24,16},{1,25},{9,1},{17,9},{25,17},{2,26},{10... | collective-permute-start | bytes 688136 | tf_op jit(solution)/shard_map/ppermute | solution.py:16
  32.9 9.1 %collective-permute-start.3 = (bf16[64,1920]{1,0:T(8,128)(2,1)S(1)}, bf16[64,1920]{1,0:T(8,128)(2,1)S(1)}, u32[]{:S(2)}, u32[]{:S(2)}) collective-permute-start(bf16[64,1920]{1,0:T(8,128)(2,1)S(1)} %slice.140), channel_id=1, source_target_pairs={{0,2},{2,4},{4,6},{6,0},{1,3},{3,5},{5,7},{7,1},{8,10},{10,12},{12... | collective-permute-start | bytes 737288 | tf_op jit(solution)/shard_map/ppermute | solution.py:16
  34.2 10.9 %collective-permute-start.2 = (bf16[64,1920]{1,0:T(8,128)(2,1)S(1)}, bf16[64,1920]{1,0:T(8,128)(2,1)S(1)}, u32[]{:S(2)}, u32[]{:S(2)}) collective-permute-start(bf16[64,1920]{1,0:T(8,128)(2,1)S(1)} %slice.140), channel_id=1, source_target_pairs={{0,4},{2,6},{4,0},{6,2},{1,5},{3,7},{5,1},{7,3},{8,12},{10,14},{12... | collective-permute-start | bytes 737288 | tf_op jit(solution)/shard_map/ppermute | solution.py:16
  40.8 25.2 %collective-permute-start.12 = (bf16[256,1792]{1,0:T(8,128)(2,1)S(1)}, bf16[256,1792]{1,0:T(8,128)(2,1)S(1)}, u32[]{:S(2)}, u32[]{:S(2)}) collective-permute-start(bf16[256,1792]{1,0:T(8,128)(2,1)S(1)} %pad_maximum_fusion.1.refs_3_.refs_5_), channel_id=1, source_target_pairs={{0,2},{2,4},{4,6},{6,0},{1,3},{3,5},{5,7},{7,1},{8,10},{10,12},{12... | collective-permute-start | bytes 2752520 | tf_op jit(solution)/shard_map/ppermute | solution.py:16
  45.2 22.8 %collective-permute-start.5 = (bf16[256,1920]{1,0:T(8,128)(2,1)S(1)}, bf16[256,1920]{1,0:T(8,128)(2,1)S(1)}, u32[]{:S(2)}, u32[]{:S(2)}) collective-permute-start(bf16[256,1920]{1,0:T(8,128)(2,1)S(1)} %pad_maximum_fusion.refs_0_), channel_id=1, source_target_pairs={{0,8},{8,16},{16,24},{24,0},{1,9},{9,17},{17,25},{25,1},{2,10},{10... | collective-permute-start | bytes 2949128 | tf_op jit(solution)/shard_map/ppermute | solution.py:16
  45.7 32.3 %collective-permute-start.4 = (bf16[256,1920]{1,0:T(8,128)(2,1)S(1)}, bf16[256,1920]{1,0:T(8,128)(2,1)}, u32[]{:S(2)}, u32[]{:S(2)}) collective-permute-start(bf16[256,1920]{1,0:T(8,128)(2,1)S(1)} %pad_maximum_fusion.refs_0_), channel_id=1, source_target_pairs={{0,24},{8,0},{16,8},{24,16},{1,25},{9,1},{17,9},{25,17},{2,26},{10... | collective-permute-start | bytes 2949128 | tf_op jit(solution)/shard_map/ppermute | solution.py:16
  48.0 36.4 %collective-permute-start.15 = (bf16[256,1920]{1,0:T(8,128)(2,1)S(1)}, bf16[256,1920]{1,0:T(8,128)(2,1)S(1)}, u32[]{:S(2)}, u32[]{:S(2)}) collective-permute-start(bf16[256,1920]{1,0:T(8,128)(2,1)S(1)} %pad_maximum_fusion.refs_0_), channel_id=1, source_target_pairs={{0,1},{1,0},{2,3},{3,2},{4,5},{5,4},{6,7},{7,6},{8,9},{9,8},{10,11... | collective-permute-start | bytes 2949128 | tf_op jit(solution)/shard_map/ppermute | solution.py:16
  54.9 22.0 %collective-permute-start.11 = (bf16[256,1792]{1,0:T(8,128)(2,1)S(1)}, bf16[256,1792]{1,0:T(8,128)(2,1)}, u32[]{:S(2)}, u32[]{:S(2)}) collective-permute-start(bf16[256,1792]{1,0:T(8,128)(2,1)S(1)} %pad_maximum_fusion.1.refs_3_.refs_5_), channel_id=1, source_target_pairs={{0,6},{2,0},{4,2},{6,4},{1,7},{3,1},{5,3},{7,5},{8,14},{10,8},{12,... | collective-permute-start | bytes 2752520 | tf_op jit(solution)/shard_map/ppermute | solution.py:16
  65.9 15.9 %collective-permute-start.20 = (bf16[256,1792]{1,0:T(8,128)(2,1)S(1)}, bf16[256,1792]{1,0:T(8,128)(2,1)S(1)}, u32[]{:S(2)}, u32[]{:S(2)}) collective-permute-start(bf16[256,1792]{1,0:T(8,128)(2,1)S(1)} %pad_maximum_fusion.1.refs_3_.refs_5_), channel_id=1, source_target_pairs={{0,1},{1,0},{2,3},{3,2},{4,5},{5,4},{6,7},{7,6},{8,9},{9,8},{10,11... | collective-permute-start | bytes 2752520 | tf_op jit(solution)/shard_map/ppermute | solution.py:16
  68.0 18.7 %collective-permute-start.13 = (bf16[128,1792]{1,0:T(8,128)(2,1)S(1)}, bf16[128,1792]{1,0:T(8,128)(2,1)S(1)}, u32[]{:S(2)}, u32[]{:S(2)}) collective-permute-start(bf16[128,1792]{1,0:T(8,128)(2,1)S(1)} %slice.144), channel_id=1, source_target_pairs={{0,2},{2,4},{4,6},{6,0},{1,3},{3,5},{5,7},{7,1},{8,10},{10,12},{12... | collective-permute-start | bytes 1376264 | tf_op jit(solution)/shard_map/ppermute | solution.py:16
  77.0 18.8 %collective-permute-start.6 = (bf16[128,1920]{1,0:T(8,128)(2,1)S(1)}, bf16[128,1920]{1,0:T(8,128)(2,1)S(1)}, u32[]{:S(2)}, u32[]{:S(2)}) collective-permute-start(bf16[128,1920]{1,0:T(8,128)(2,1)S(1)} %slice.141), channel_id=1, source_target_pairs={{0,8},{8,16},{16,24},{24,0},{1,9},{9,17},{17,25},{25,1},{2,10},{10... | collective-permute-start | bytes 1474568 | tf_op jit(solution)/shard_map/ppermute | solution.py:16
  79.1 16.7 %collective-permute-start.7 = (bf16[128,1920]{1,0:T(8,128)(2,1)S(1)}, bf16[128,1920]{1,0:T(8,128)(2,1)}, u32[]{:S(2)}, u32[]{:S(2)}) collective-permute-start(bf16[128,1920]{1,0:T(8,128)(2,1)S(1)} %slice.142), channel_id=1, source_target_pairs={{0,24},{8,0},{16,8},{24,16},{1,25},{9,1},{17,9},{25,17},{2,26},{10... | collective-permute-start | bytes 1474568 | tf_op jit(solution)/shard_map/ppermute | solution.py:16
  82.8 10.7 %collective-permute-start.14 = (bf16[128,1792]{1,0:T(8,128)(2,1)S(1)}, bf16[128,1792]{1,0:T(8,128)(2,1)S(1)}, u32[]{:S(2)}, u32[]{:S(2)}) collective-permute-start(bf16[128,1792]{1,0:T(8,128)(2,1)S(1)} %slice.145), channel_id=1, source_target_pairs={{0,6},{2,0},{4,2},{6,4},{1,7},{3,1},{5,3},{7,5},{8,14},{10,8},{12,... | collective-permute-start | bytes 1376264 | tf_op jit(solution)/shard_map/ppermute | solution.py:16
  85.3 12.7 %collective-permute-start.22 = (bf16[256,1792]{1,0:T(8,128)(2,1)S(1)}, bf16[256,1792]{1,0:T(8,128)(2,1)S(1)}, u32[]{:S(2)}, u32[]{:S(2)}) collective-permute-start(bf16[256,1792]{1,0:T(8,128)(2,1)S(1)} %collective-permute-done.12.refs_5_.refs_7_), channel_id=1, source_target_pairs={{0,1},{1,0},{2,3},{3,2},{4,5},{5,4},{6,7},{7,6},{8,9},{9,8},{10,11... | collective-permute-start | bytes 2752520 | tf_op jit(solution)/shard_map/ppermute | solution.py:16
  86.7 10.4 %collective-permute-start.23 = (bf16[128,1792]{1,0:T(8,128)(2,1)S(1)}, bf16[128,1792]{1,0:T(8,128)(2,1)S(1)}, u32[]{:S(2)}, u32[]{:S(2)}) collective-permute-start(bf16[128,1792]{1,0:T(8,128)(2,1)S(1)} %collective-permute-done.13.refs_8_), channel_id=1, source_target_pairs={{0,1},{1,0},{2,3},{3,2},{4,5},{5,4},{6,7},{7,6},{8,9},{9,8},{10,11... | collective-permute-start | bytes 1376264 | tf_op jit(solution)/shard_map/ppermute | solution.py:16
  93.5 16.3 %collective-permute-start.17 = (bf16[256,1920]{1,0:T(8,128)(2,1)S(1)}, bf16[256,1920]{1,0:T(8,128)(2,1)S(1)}, u32[]{:S(2)}, u32[]{:S(2)}) collective-permute-start(bf16[256,1920]{1,0:T(8,128)(2,1)S(1)} %collective-permute-done.5.refs_2_), channel_id=1, source_target_pairs={{0,1},{1,0},{2,3},{3,2},{4,5},{5,4},{6,7},{7,6},{8,9},{9,8},{10,11... | collective-permute-start | bytes 2949128 | tf_op jit(solution)/shard_map/ppermute | solution.py:16
  95.8 14.0 %collective-permute-start.16 = (bf16[256,1920]{1,0:T(8,128)(2,1)}, bf16[256,1920]{1,0:T(8,128)(2,1)}, u32[]{:S(2)}, u32[]{:S(2)}) collective-permute-start(bf16[256,1920]{1,0:T(8,128)(2,1)} %collective-permute-done.4.refs_1_), channel_id=1, source_target_pairs={{0,1},{1,0},{2,3},{3,2},{4,5},{5,4},{6,7},{7,6},{8,9},{9,8},{10,11... | collective-permute-start | bytes 2949128 | tf_op jit(solution)/shard_map/ppermute | solution.py:16
  97.9 11.9 %collective-permute-start.21 = (bf16[256,1792]{1,0:T(8,128)(2,1)}, bf16[256,1792]{1,0:T(8,128)(2,1)}, u32[]{:S(2)}, u32[]{:S(2)}) collective-permute-start(bf16[256,1792]{1,0:T(8,128)(2,1)} %collective-permute-done.11.refs_4_.refs_6_), channel_id=1, source_target_pairs={{0,1},{1,0},{2,3},{3,2},{4,5},{5,4},{6,7},{7,6},{8,9},{9,8},{10,11... | collective-permute-start | bytes 2752520 | tf_op jit(solution)/shard_map/ppermute | solution.py:16
  98.9 10.9 %collective-permute-start.18 = (bf16[128,1920]{1,0:T(8,128)(2,1)S(1)}, bf16[128,1920]{1,0:T(8,128)(2,1)}, u32[]{:S(2)}, u32[]{:S(2)}) collective-permute-start(bf16[128,1920]{1,0:T(8,128)(2,1)S(1)} %collective-permute-done.6.refs_3_), channel_id=1, source_target_pairs={{0,1},{1,0},{2,3},{3,2},{4,5},{5,4},{6,7},{7,6},{8,9},{9,8},{10,11... | collective-permute-start | bytes 1474568 | tf_op jit(solution)/shard_map/ppermute | solution.py:16
  100.8 9.0 %collective-permute-start.19 = (bf16[128,1920]{1,0:T(8,128)(2,1)}, bf16[128,1920]{1,0:T(8,128)(2,1)}, u32[]{:S(2)}, u32[]{:S(2)}) collective-permute-start(bf16[128,1920]{1,0:T(8,128)(2,1)} %collective-permute-done.7.refs_4_), channel_id=1, source_target_pairs={{0,1},{1,0},{2,3},{3,2},{4,5},{5,4},{6,7},{7,6},{8,9},{9,8},{10,11... | collective-permute-start | bytes 1474568 | tf_op jit(solution)/shard_map/ppermute | solution.py:16
  135.0 20.4 %collective-permute-start.25 = (bf16[3,2,4,64,1792]{4,3,2,1,0:T(8,128)(2,1)S(1)}, bf16[3,2,4,64,1792]{4,3,2,1,0:T(8,128)(2,1)S(1)}, u32[]{:S(2)}, u32[]{:S(2)}) collective-permute-start(bf16[3,2,4,64,1792]{4,3,2,1,0:T(8,128)(2,1)S(1)} %down_send.1), channel_id=1, source_target_pairs={{0,1},{1,0},{2,3},{3,2},{4,5},{5,4},{6,7},{7,6},{8,9},{9,8},{10,11... | collective-permute-start | bytes 16515080 | tf_op jit(solution)/shard_map/ppermute | solution.py:16
  135.2 11.5 %collective-permute-start.26 = (bf16[1,2,4,64,1792]{4,3,2,1,0:T(8,128)(2,1)S(1)}, bf16[1,2,4,64,1792]{4,3,2,1,0:T(8,128)(2,1)S(1)}, u32[]{:S(2)}, u32[]{:S(2)}) collective-permute-start(bf16[1,2,4,64,1792]{4,3,2,1,0:T(8,128)(2,1)S(1)} %get-tuple-element.20), channel_id=1, source_target_pairs={{0,1},{1,0},{2,3},{3,2},{4,5},{5,4},{6,7},{7,6},{8,9},{9,8},{10,11... | collective-permute-start | bytes 5505032 | tf_op jit(solution)/shard_map/ppermute | solution.py:16
  149.9 12.5 %collective-permute-start.36 = (bf16[2,64,1792]{2,1,0:T(8,128)(2,1)S(1)}, bf16[2,64,1792]{2,1,0:T(8,128)(2,1)S(1)}, u32[]{:S(2)}, u32[]{:S(2)}) collective-permute-start(bf16[2,64,1792]{2,1,0:T(8,128)(2,1)S(1)} %get-tuple-element.28), channel_id=1, source_target_pairs={{0,6},{2,0},{4,2},{6,4},{1,7},{3,1},{5,3},{7,5},{8,14},{10,8},{12,... | collective-permute-start | bytes 1376264 | tf_op jit(solution)/shard_map/ppermute | solution.py:16
  152.7 15.9 %collective-permute-start.27 = (bf16[2,64,1792]{2,1,0:T(8,128)(2,1)S(1)}, bf16[2,64,1792]{2,1,0:T(8,128)(2,1)S(1)}, u32[]{:S(2)}, u32[]{:S(2)}) collective-permute-start(bf16[2,64,1792]{2,1,0:T(8,128)(2,1)S(1)} %get-tuple-element.21), channel_id=1, source_target_pairs={{0,8},{8,16},{16,24},{24,0},{1,9},{9,17},{17,25},{25,1},{2,10},{10... | collective-permute-start | bytes 1376264 | tf_op jit(solution)/shard_map/ppermute | solution.py:16
  152.7 15.3 %collective-permute-start.29 = (bf16[2,64,1792]{2,1,0:T(8,128)(2,1)S(1)}, bf16[2,64,1792]{2,1,0:T(8,128)(2,1)S(1)}, u32[]{:S(2)}, u32[]{:S(2)}) collective-permute-start(bf16[2,64,1792]{2,1,0:T(8,128)(2,1)S(1)} %get-tuple-element.23), channel_id=1, source_target_pairs={{0,24},{8,0},{16,8},{24,16},{1,25},{9,1},{17,9},{25,17},{2,26},{10... | collective-permute-start | bytes 1376264 | tf_op jit(solution)/shard_map/ppermute | solution.py:16
  155.4 12.3 %collective-permute-start.34 = (bf16[2,64,1792]{2,1,0:T(8,128)(2,1)S(1)}, bf16[2,64,1792]{2,1,0:T(8,128)(2,1)S(1)}, u32[]{:S(2)}, u32[]{:S(2)}) collective-permute-start(bf16[2,64,1792]{2,1,0:T(8,128)(2,1)S(1)} %get-tuple-element.26), channel_id=1, source_target_pairs={{0,2},{2,4},{4,6},{6,0},{1,3},{3,5},{5,7},{7,1},{8,10},{10,12},{12... | collective-permute-start | bytes 1376264 | tf_op jit(solution)/shard_map/ppermute | solution.py:16
  162.7 22.2 %collective-permute-start.37 = (bf16[4,64,1792]{2,1,0:T(8,128)(2,1)S(1)}, bf16[4,64,1792]{2,1,0:T(8,128)(2,1)S(1)}, u32[]{:S(2)}, u32[]{:S(2)}) collective-permute-start(bf16[4,64,1792]{2,1,0:T(8,128)(2,1)S(1)} %pad_maximum_fusion.5), channel_id=1, source_target_pairs={{0,6},{2,0},{4,2},{6,4},{1,7},{3,1},{5,3},{7,5},{8,14},{10,8},{12,... | collective-permute-start | bytes 2752520 | tf_op jit(solution)/shard_map/ppermute | solution.py:16
  167.9 21.4 %collective-permute-start.35 = (bf16[4,64,1792]{2,1,0:T(8,128)(2,1)S(1)}, bf16[4,64,1792]{2,1,0:T(8,128)(2,1)S(1)}, u32[]{:S(2)}, u32[]{:S(2)}) collective-permute-start(bf16[4,64,1792]{2,1,0:T(8,128)(2,1)S(1)} %pad_maximum_fusion.4), channel_id=1, source_target_pairs={{0,2},{2,4},{4,6},{6,0},{1,3},{3,5},{5,7},{7,1},{8,10},{10,12},{12... | collective-permute-start | bytes 2752520 | tf_op jit(solution)/shard_map/ppermute | solution.py:16
  168.3 24.2 %collective-permute-start.30 = (bf16[4,64,1792]{2,1,0:T(8,128)(2,1)S(1)}, bf16[4,64,1792]{2,1,0:T(8,128)(2,1)S(1)}, u32[]{:S(2)}, u32[]{:S(2)}) collective-permute-start(bf16[4,64,1792]{2,1,0:T(8,128)(2,1)S(1)} %pad_maximum_fusion.3), channel_id=1, source_target_pairs={{0,24},{8,0},{16,8},{24,16},{1,25},{9,1},{17,9},{25,17},{2,26},{10... | collective-permute-start | bytes 2752520 | tf_op jit(solution)/shard_map/ppermute | solution.py:16
  168.9 23.6 %collective-permute-start.28 = (bf16[4,64,1792]{2,1,0:T(8,128)(2,1)S(1)}, bf16[4,64,1792]{2,1,0:T(8,128)(2,1)S(1)}, u32[]{:S(2)}, u32[]{:S(2)}) collective-permute-start(bf16[4,64,1792]{2,1,0:T(8,128)(2,1)S(1)} %pad_maximum_fusion.2), channel_id=1, source_target_pairs={{0,8},{8,16},{16,24},{24,0},{1,9},{9,17},{17,25},{25,1},{2,10},{10... | collective-permute-start | bytes 2752520 | tf_op jit(solution)/shard_map/ppermute | solution.py:16
  217.4 10.9 %collective-permute-start.41 = (bf16[4,3584]{1,0:T(4,128)(2,1)S(1)}, bf16[4,3584]{1,0:T(4,128)(2,1)S(1)}, u32[]{:S(2)}, u32[]{:S(2)}) collective-permute-start(bf16[4,3584]{1,0:T(4,128)(2,1)S(1)} %get-tuple-element.36), channel_id=1, source_target_pairs={{0,1},{1,0},{2,3},{3,2},{4,5},{5,4},{6,7},{7,6},{8,9},{9,8},{10,11... | collective-permute-start | bytes 86024 | tf_op jit(solution)/shard_map/ppermute | solution.py:16
  (31 other events, 217.8 us)
